TPU v7x, 8 devices: a whole 2x2x1 slice. The times are simulated.
8 devices in a mesh: rep: 1 (over z), mp: 2 (over y), tok: 4 (over x, core).
Axes of the slice: x: 2, y: 2, z: 1, core: 2. Of those that a mesh axis runs over, the one named last changes fastest.
Arguments:
- hidden_in: bfloat16 [16384, 768], P(('rep', 'tok', 'mp'))
- seg_ids: int32 [16384], P(('rep', 'tok', 'mp'))
- expert_ids: int32 [16384, 2], P(('rep', 'tok', 'mp'))
- expert_gates: float32 [16384, 2], P(('rep', 'tok', 'mp'))
- w_query: bfloat16 [2, 768, 12, 64], P(None, 'tok', 'mp')
- w_key: bfloat16 [2, 768, 12, 64], P(None, 'tok', 'mp')
- w_value: bfloat16 [2, 768, 12, 64], P(None, 'tok', 'mp')
- w_out: bfloat16 [2, 12, 64, 768], P(None, 'mp', None, 'tok')
- w_gate: bfloat16 [2, 32, 768, 3072], P(None, None, 'tok', 'mp')
- w_up: bfloat16 [2, 32, 768, 3072], P(None, None, 'tok', 'mp')
- w_down: bfloat16 [2, 32, 3072, 768], P(None, None, 'mp', 'tok')
- gain_attn: bfloat16 [2, 768], replicated
- gain_mlp: bfloat16 [2, 768], replicated
Outputs:
- output: float32 [16384, 768], P(('rep', 'tok', 'mp'))
All inputs are finite; a program needn't handle non-finite values.
Results may differ from a plain program's by a relative error of at most 0.00981009.
Values are sent between devices in bfloat16 or wider.
A program may use at most 1 GiB of HBM per device.

v0:
```python
import jax
import jax.numpy as jnp
from jax import lax
from jax.sharding import PartitionSpec as P

EPS = 1e-5
ROPE_BASE = 10000.0


def rms_norm(residual, gain):
    inv_rms = lax.rsqrt(jnp.mean(residual * residual, axis=-1, keepdims=True) + EPS)
    return (residual * inv_rms * gain.astype(jnp.float32)).astype(jnp.bfloat16)


def request_positions(seg_rows):
    token_index = jnp.arange(seg_rows.shape[-1], dtype=jnp.int32)
    is_start = jnp.concatenate([jnp.ones(seg_rows.shape[:-1] + (1,), dtype=jnp.bool_), seg_rows[..., 1:] != seg_rows[..., :-1]], axis=-1)
    start_index = lax.cummax(jnp.where(is_start, token_index, 0), axis=seg_rows.ndim - 1)
    return token_index - start_index


def rope_tables(positions, head_dim):
    inv_freq = jnp.power(ROPE_BASE, -jnp.arange(head_dim // 2, dtype=jnp.float32) * 2.0 / head_dim)
    angles = positions.astype(jnp.float32)[..., None] * inv_freq
    return jnp.cos(angles)[..., None, :], jnp.sin(angles)[..., None, :]


def apply_rope(vectors, cosines, sines):
    half_dim = vectors.shape[-1] // 2
    first_half = vectors[..., :half_dim]
    second_half = vectors[..., half_dim:]
    return jnp.concatenate([first_half * cosines - second_half * sines, second_half * cosines + first_half * sines], axis=-1)


def block_attention(q_rot, k_rot, v_all, seg_query, query_index, seg_keys, key_index):
    n_query, kv_heads, groups, head_dim = q_rot.shape
    block = min(n_query, 512)
    num_blocks = n_query // block
    scale = head_dim ** -0.5

    def one_block(block_in):
        q_block, seg_block, index_block = block_in
        scores = jnp.einsum('bhgd,shd->hgbs', q_block, k_rot, preferred_element_type=jnp.float32) * scale
        allowed = (seg_block[:, None] == seg_keys[None, :]) & (key_index[None, :] <= index_block[:, None])
        attn_prob = jax.nn.softmax(jnp.where(allowed, scores, -1e30), axis=-1).astype(jnp.bfloat16)
        return jnp.einsum('hgbs,shd->bhgd', attn_prob, v_all, preferred_element_type=jnp.float32).astype(jnp.bfloat16)

    block_outs = lax.map(one_block, (q_rot.reshape(num_blocks, block, kv_heads, groups, head_dim), seg_query.reshape(num_blocks, block), query_index.reshape(num_blocks, block)))
    return block_outs.reshape(n_query, kv_heads * groups, head_dim)


def expert_mix(normed, pair_token, pair_gate, group_sizes, gate_weight, up_weight, down_weight):
    pair_rows = normed[pair_token]
    gate_pre = lax.ragged_dot(pair_rows, gate_weight, group_sizes, preferred_element_type=jnp.float32)
    up_pre = lax.ragged_dot(pair_rows, up_weight, group_sizes, preferred_element_type=jnp.float32)
    hidden_act = (jax.nn.silu(gate_pre) * up_pre).astype(jnp.bfloat16)
    down_out = lax.ragged_dot(hidden_act, down_weight, group_sizes, preferred_element_type=jnp.float32)
    return jax.ops.segment_sum(down_out * pair_gate[:, None], pair_token, num_segments=normed.shape[0])


def solution(mesh):
    token_spec = P(('rep', 'tok', 'mp'))
    row_spec = P(('rep', 'tok', 'mp'), None)
    head_weight = P(None, 'tok', 'mp', None)
    in_specs = (row_spec, token_spec, row_spec, row_spec, head_weight, head_weight, head_weight, P(None, 'mp', None, 'tok'), P(None, None, 'tok', 'mp'), P(None, None, 'tok', 'mp'), P(None, None, 'mp', 'tok'), P(None, None), P(None, None))

    def device_step(hidden_in, seg_ids, expert_ids, expert_gates, w_query, w_key, w_value, w_out, w_gate, w_up, w_down, gain_attn, gain_mlp):
        num_layers, _, q_local, head_dim = w_query.shape
        kv_local = w_key.shape[2]
        groups = q_local // kv_local
        num_experts = w_gate.shape[1]
        seg_full = lax.all_gather(seg_ids, 'mp', axis=0, tiled=True)
        ids_full = lax.all_gather(expert_ids, 'mp', axis=0, tiled=True)
        gates_full = lax.all_gather(expert_gates, 'mp', axis=0, tiled=True)
        seq_len = seg_full.shape[0]
        token_index = jnp.arange(seq_len, dtype=jnp.int32)
        cosines, sines = rope_tables(request_positions(seg_full), head_dim)
        flat_ids = ids_full.reshape(2 * seq_len)
        pair_order = jnp.argsort(flat_ids, stable=True)
        group_sizes = jnp.bincount(flat_ids, length=num_experts).astype(jnp.int32)
        pair_token = pair_order // 2
        pair_gate = gates_full.reshape(2 * seq_len)[pair_order]
        residual = hidden_in.astype(jnp.float32)
        for layer in range(num_layers):
            q_weight = lax.all_gather(w_query[layer], 'tok', axis=0, tiled=True)
            k_weight = lax.all_gather(w_key[layer], 'tok', axis=0, tiled=True)
            v_weight = lax.all_gather(w_value[layer], 'tok', axis=0, tiled=True)
            o_weight = lax.all_gather(w_out[layer], 'tok', axis=2, tiled=True)
            gate_weight = lax.all_gather(w_gate[layer], 'tok', axis=1, tiled=True)
            up_weight = lax.all_gather(w_up[layer], 'tok', axis=1, tiled=True)
            down_weight = lax.all_gather(w_down[layer], 'tok', axis=2, tiled=True)
            normed = lax.all_gather(rms_norm(residual, gain_attn[layer]), 'mp', axis=0, tiled=True)
            q_proj = jnp.einsum('se,ehd->shd', normed, q_weight, preferred_element_type=jnp.float32)
            k_proj = jnp.einsum('se,ehd->shd', normed, k_weight, preferred_element_type=jnp.float32)
            v_proj = jnp.einsum('se,ehd->shd', normed, v_weight, preferred_element_type=jnp.float32)
            q_rot = apply_rope(q_proj, cosines, sines).astype(jnp.bfloat16).reshape(seq_len, kv_local, groups, head_dim)
            k_rot = apply_rope(k_proj, cosines, sines).astype(jnp.bfloat16)
            attn_out = block_attention(q_rot, k_rot, v_proj.astype(jnp.bfloat16), seg_full, token_index, seg_full, token_index)
            attn_part = jnp.einsum('shd,hde->se', attn_out, o_weight, preferred_element_type=jnp.float32)
            residual = residual + lax.psum_scatter(attn_part, 'mp', scatter_dimension=0, tiled=True)
            normed = lax.all_gather(rms_norm(residual, gain_mlp[layer]), 'mp', axis=0, tiled=True)
            mix_part = expert_mix(normed, pair_token, pair_gate, group_sizes, gate_weight, up_weight, down_weight)
            residual = residual + lax.psum_scatter(mix_part, 'mp', scatter_dimension=0, tiled=True)
        return residual

    return jax.shard_map(device_step, mesh=mesh, in_specs=in_specs, out_specs=row_spec, check_vma=False)
```

profile of v0, /device:TPU:0, one launch (start us, length us, event | category | flops | bytes accessed | tf_op | source)
XLA Modules:
  0.0 5304.6 jit_solution(15326285813689265243)
XLA Ops:
  129.5 553.0 %while.22 = (s32[]{:T(128)}, bf16[8,512,6,1,64]{1,4,2,3,0:T(8,128)(2,1)}, s32[8,512]{1,0:T(8,128)S(1)}, s32[4096]{0:T(1024)S(1)}, s32[8,512]{1,0:T(8,128)S(1)}, ...) while((s32[]{:T(128)}, ...), condition=%wide.region_6.7_spmd.clone, body=%wide.region_3.6_spmd.clone.sunk | while | flops 3378702336 | bytes 166552688 | solution.py:48
  701.5 142.0 %reduce-scatter.5.cloned.1.call-done = f32[2048,768]{1,0:T(8,128)} async-done(((f32[4096,768]{1,0:T(8,128)}), f32[2048,768]{1,0:T(8,128)}) %reduce-scatter.5.cloned.1.call-update) | async-done | bytes 6291472 | tf_op jit(solution)/shard_map/reduce_scatter | solution.py:100
  956.2 57.5 %scatter_custom_fusion = s32[32]{0:T(128)} fusion(s32[8192]{0:T(1024)S(1)} %reshape.312, s32[8192]{0:T(1024)S(1)} %ne.20, s32[]{:T(128)} %copy.89), kind=kCustom, calls=%fused_computation.117 | custom fusion | flops 8192 | bytes 132 | tf_op jit(solution)/shard_map/scatter-add | solution.py:80
  1030.0 80.4 %gather_fusion.1 = f32[8192]{0:T(1024)} fusion(f32[8192]{0:T(1024)S(1)} %reshape.280, s32[8192]{0:T(1024)S(1)} %get-tuple-element.237), kind=kCustom, calls=%fused_computation.1 | custom fusion | bytes 98304 | tf_op jit(solution)/shard_map/gather | solution.py:82
  1151.0 217.3 %all-gather.33.cloned.1.call-done = bf16[1,32,768,1536]{3,2,1,0:T(8,128)(2,1)} async-done(((bf16[1,32,192,1536]{3,2,1,0:T(8,128)(2,1)}), bf16[1,32,768,1536]{3,2,1,0:T(8,128)(2,1)}) %all-gather.33.cloned.1.call-update) | async-done | bytes 75497488 | tf_op jit(solution)/shard_map/all_gather | solution.py:89
  1368.3 95.1 %ragged-dot-none.5 = f32[8192,1536]{1,0:T(8,128)} custom-call(s32[1]{0:T(128)} %get-tuple-element.115, s32[33]{0:T(128)} %get-tuple-element.116, s32[63]{0:T(128)} %get-tuple-element.117, s32[63]{0:T(128)} %get-tuple-element.118, s32[1]{0:T(128)} %get-tuple-element.115, bf16[8192,768]{1,0:T(8,128)(2,1)} %gather_fusion, bf16[32,768,1536]{2,1,0:T(8,128)(2,1)} %bitcast.13), custom_call_target="tpu_custom_call" | custom-call | flops 19327352832 | bytes 138412160 | tf_op jit(solution)/shard_map/ragged_dot_general/ragged-dot-none
  1463.4 344.5 %all-gather.35.cloned.1.call-done = bf16[1,32,768,1536]{3,2,1,0:T(8,128)(2,1)} async-done(((bf16[1,32,192,1536]{3,2,1,0:T(8,128)(2,1)}), bf16[1,32,768,1536]{3,2,1,0:T(8,128)(2,1)}) %all-gather.35.cloned.1.call-update) | async-done | bytes 75497488 | tf_op jit(solution)/shard_map/all_gather | solution.py:90
  1807.9 95.5 %ragged-dot-none.4 = f32[8192,1536]{1,0:T(8,128)} custom-call(s32[1]{0:T(128)} %get-tuple-element.115, s32[33]{0:T(128)} %get-tuple-element.116, s32[63]{0:T(128)} %get-tuple-element.117, s32[63]{0:T(128)} %get-tuple-element.118, s32[1]{0:T(128)} %get-tuple-element.115, bf16[8192,768]{1,0:T(8,128)(2,1)} %gather_fusion, bf16[32,768,1536]{2,1,0:T(8,128)(2,1)} %bitcast.14), custom_call_target="tpu_custom_call" | custom-call | flops 19327352832 | bytes 138412160 | tf_op jit(solution)/shard_map/ragged_dot_general/ragged-dot-none
  1943.9 303.7 %all-gather.37.cloned.1.call-done = bf16[1,32,1536,768]{2,1,0,3:T(8,128)(2,1)} async-done(((bf16[1,32,1536,192]{2,1,0,3:T(8,128)(2,1)}), bf16[1,32,1536,768]{2,1,0,3:T(8,128)(2,1)}) %all-gather.37.cloned.1.call-update) | async-done | bytes 75497488 | tf_op jit(solution)/shard_map/all_gather | solution.py:91
  2247.6 92.3 %copy.45 = bf16[1,32,1536,768]{3,2,1,0:T(8,128)(2,1)} copy(bf16[1,32,1536,768]{2,1,0,3:T(8,128)(2,1)} %all-gather.37.cloned.1.call-done) | data formatting | bytes 150994944 | tf_op jit(solution)/shard_map/all_gather | solution.py:91
  2339.9 87.3 %ragged-dot-none.3 = f32[8192,768]{1,0:T(8,128)} custom-call(s32[1]{0:T(128)} %get-tuple-element.115, s32[33]{0:T(128)} %get-tuple-element.116, s32[63]{0:T(128)} %get-tuple-element.117, s32[63]{0:T(128)} %get-tuple-element.118, s32[1]{0:T(128)} %get-tuple-element.115, bf16[8192,1536]{1,0:T(8,128)(2,1)} %multiply_convert_fusion.1, ...), custom_call_target="tpu_custom_call" | custom-call | flops 19327352832 | bytes 125829248 | tf_op jit(solution)/shard_map/ragged_dot_general/ragged-dot-none
  2427.2 63.3 %scatter_custom_fusion.1 = f32[4096,768]{1,0:T(8,128)} fusion(s32[8192]{0:T(1024)} %get-tuple-element.239, f32[8192,768]{1,0:T(8,128)} %ragged-dot-none.3, f32[8192]{0:T(1024)S(1)} %copy-done.19, f32[]{:T(128)} %constant.82.clone.1), kind=kCustom, calls=%fused_computation.52 | custom fusion | flops 12582912 | bytes 37782016 | tf_op jit(solution)/shard_map/scatter-add | solution.py:58
  2490.6 142.1 %reduce-scatter.7.cloned.1.call-done = f32[2048,768]{1,0:T(8,128)} async-done(((f32[4096,768]{1,0:T(8,128)}), f32[2048,768]{1,0:T(8,128)}) %reduce-scatter.7.cloned.1.call-update) | async-done | bytes 6291472 | tf_op jit(solution)/shard_map/reduce_scatter | solution.py:103
  2744.5 558.5 %while.23 = (s32[]{:T(128)}, bf16[8,512,6,1,64]{1,4,2,3,0:T(8,128)(2,1)}, s32[8,512]{1,0:T(8,128)}, s32[4096]{0:T(1024)S(1)}, s32[8,512]{1,0:T(8,128)}, /*index=...) while((s32[]{:T(128)}, ...), condition=%wide.region_17.18_spmd.clone, body=%wide.region_14.17_spmd.clone.sunk | while | flops 3378702336 | bytes 166552688 | solution.py:48
  3341.2 121.6 %reduce-scatter.9.cloned.1.call-done = f32[2048,768]{1,0:T(8,128)} async-done(((f32[4096,768]{1,0:T(8,128)}), f32[2048,768]{1,0:T(8,128)}) %reduce-scatter.9.cloned.1.call-update) | async-done | bytes 6291472 | tf_op jit(solution)/shard_map/reduce_scatter | solution.py:100
  3474.8 427.9 %all-gather.43.cloned.1.call-done = bf16[1,32,1536,768]{2,1,0,3:T(8,128)(2,1)} async-done(((bf16[1,32,1536,192]{2,1,0,3:T(8,128)(2,1)}), bf16[1,32,1536,768]{2,1,0,3:T(8,128)(2,1)}) %all-gather.43.cloned.1.call-update) | async-done | bytes 75497488 | tf_op jit(solution)/shard_map/all_gather | solution.py:91
  3902.6 92.5 %copy.59 = bf16[1,32,1536,768]{3,2,1,0:T(8,128)(2,1)} copy(bf16[1,32,1536,768]{2,1,0,3:T(8,128)(2,1)} %all-gather.43.cloned.1.call-done) | data formatting | bytes 150994944 | tf_op jit(solution)/shard_map/all_gather | solution.py:91
  4035.8 386.2 %all-gather.39.cloned.1.call-done = bf16[1,32,768,1536]{3,2,1,0:T(8,128)(2,1)} async-done(((bf16[1,32,192,1536]{3,2,1,0:T(8,128)(2,1)}), bf16[1,32,768,1536]{3,2,1,0:T(8,128)(2,1)}) %all-gather.39.cloned.1.call-update) | async-done | bytes 75497488 | tf_op jit(solution)/shard_map/all_gather | solution.py:89
  4422.0 95.1 %ragged-dot-none.2 = f32[8192,1536]{1,0:T(8,128)} custom-call(s32[1]{0:T(128)} %get-tuple-element.115, s32[33]{0:T(128)} %get-tuple-element.116, s32[63]{0:T(128)} %get-tuple-element.117, s32[63]{0:T(128)} %get-tuple-element.118, s32[1]{0:T(128)} %get-tuple-element.115, bf16[8192,768]{1,0:T(8,128)(2,1)} %gather_fusion.2, bf16[32,768,1536]{2,1,0:T(8,128)(2,1)} %bitcast.27), custom_call_target="tpu_custom_call" | custom-call | flops 19327352832 | bytes 138412160 | tf_op jit(solution)/shard_map/ragged_dot_general/ragged-dot-none
  4517.0 344.6 %all-gather.41.cloned.1.call-done = bf16[1,32,768,1536]{3,2,1,0:T(8,128)(2,1)} async-done(((bf16[1,32,192,1536]{3,2,1,0:T(8,128)(2,1)}), bf16[1,32,768,1536]{3,2,1,0:T(8,128)(2,1)}) %all-gather.41.cloned.1.call-update) | async-done | bytes 75497488 | tf_op jit(solution)/shard_map/all_gather | solution.py:90
  4861.7 95.0 %ragged-dot-none.1 = f32[8192,1536]{1,0:T(8,128)} custom-call(s32[1]{0:T(128)} %get-tuple-element.115, s32[33]{0:T(128)} %get-tuple-element.116, s32[63]{0:T(128)} %get-tuple-element.117, s32[63]{0:T(128)} %get-tuple-element.118, s32[1]{0:T(128)} %get-tuple-element.115, bf16[8192,768]{1,0:T(8,128)(2,1)} %gather_fusion.2, bf16[32,768,1536]{2,1,0:T(8,128)(2,1)} %bitcast.28), custom_call_target="tpu_custom_call" | custom-call | flops 19327352832 | bytes 138412160 | tf_op jit(solution)/shard_map/ragged_dot_general/ragged-dot-none
  4997.5 87.2 %ragged-dot-none = f32[8192,768]{1,0:T(8,128)} custom-call(s32[1]{0:T(128)} %get-tuple-element.115, s32[33]{0:T(128)} %get-tuple-element.116, s32[63]{0:T(128)} %get-tuple-element.117, s32[63]{0:T(128)} %get-tuple-element.118, s32[1]{0:T(128)} %get-tuple-element.115, bf16[8192,1536]{1,0:T(8,128)(2,1)} %multiply_convert_fusion, bf16[32,1536,768]{2,1,0:T(8,128)(2,1)} %bitcast.29), custom_call_target="tpu_custom_call" | custom-call | flops 19327352832 | bytes 125829248 | tf_op jit(solution)/shard_map/ragged_dot_general/ragged-dot-none
  5084.7 63.2 %scatter_custom_fusion.2 = f32[4096,768]{1,0:T(8,128)} fusion(s32[8192]{0:T(1024)} %get-tuple-element.239, f32[8192,768]{1,0:T(8,128)} %ragged-dot-none, f32[8192]{0:T(1024)S(1)} %copy-done.20, f32[]{:T(128)} %constant.82.clone.1), kind=kCustom, calls=%fused_computation.50 | custom fusion | flops 12582912 | bytes 37782016 | tf_op jit(solution)/shard_map/scatter-add | solution.py:58
  5148.0 141.8 %reduce-scatter.11.cloned.1.call-done = f32[2048,768]{1,0:T(8,128)} async-done(((f32[4096,768]{1,0:T(8,128)}), f32[2048,768]{1,0:T(8,128)}) %reduce-scatter.11.cloned.1.call-update) | async-done | bytes 6291472 | tf_op jit(solution)/shard_map/reduce_scatter | solution.py:103
  (286 shorter events, 1713.1 us)
Async XLA Ops:
  6.5 100.2 %all-gather.25.cloned.1.call-start = ((), (), s32[]{:S(2)}) async-start(), calls=%async_computation.4 | async-start | bytes 9437184 | tf_op jit(solution)/shard_map/all_gather | solution.py:92
  15.0 828.5 %reduce-scatter.5.cloned.1.call-start = ((), (), s32[]{:S(2)}) async-start(), calls=%async_computation.5 | async-start | bytes 18874368 | tf_op jit(solution)/shard_map/reduce_scatter | solution.py:100
  700.2 143.3 %copy-start = (bf16[2048,768]{1,0:T(8,128)(2,1)S(1)}, bf16[2048,768]{1,0:T(8,128)(2,1)}, u32[]{:S(2)}) copy-start(bf16[2048,768]{1,0:T(8,128)(2,1)} %param.17) | copy-start | bytes 9437188
  700.2 410.1 %all-gather.27.cloned.1.call-start = ((), (), s32[]{:S(2)}) async-start(), calls=%async_computation.6 | async-start | bytes 9437184 | tf_op jit(solution)/shard_map/all_gather | solution.py:101
  850.3 518.0 %all-gather.33.cloned.1.call-start = ((), (), s32[]{:S(2)}) async-start(), calls=%async_computation.12 | async-start | bytes 94371840 | tf_op jit(solution)/shard_map/all_gather | solution.py:89
  875.8 932.1 %all-gather.35.cloned.1.call-start = ((), (), s32[]{:S(2)}) async-start(), calls=%async_computation.13 | async-start | bytes 94371840 | tf_op jit(solution)/shard_map/all_gather | solution.py:90
  901.2 1346.5 %all-gather.37.cloned.1.call-start = ((), (), s32[]{:S(2)}) async-start(), calls=%async_computation.14 | async-start | bytes 94371840 | tf_op jit(solution)/shard_map/all_gather | solution.py:91
  947.1 69.2 %copy-start.28 = (f32[2048,2]{0,1:T(2,128)S(1)}, f32[2048,2]{0,1:T(2,128)}, u32[]{:S(2)}) copy-start(f32[2048,2]{0,1:T(2,128)} %param.20) | copy-start | bytes 49156
  947.1 1685.5 %reduce-scatter.7.cloned.1.call-start = ((), (), s32[]{:S(2)}) async-start(), calls=%async_computation.7 | async-start | bytes 18874368 | tf_op jit(solution)/shard_map/reduce_scatter | solution.py:103
  1030.0 80.4 %copy-start.21 = (s32[8192]{0:T(1024)}, s32[8192]{0:T(1024)S(1)}, u32[]{:S(2)}) copy-start(s32[8192]{0:T(1024)S(1)} %get-tuple-element.238) | copy-start | bytes 98308
  2339.9 87.3 %copy-start.19 = (f32[8192]{0:T(1024)S(1)}, f32[8192]{0:T(1024)}, u32[]{:S(2)}) copy-start(f32[8192]{0:T(1024)} %gather_fusion.1) | copy-start | bytes 98308
  2490.5 142.2 %copy-start.1 = (bf16[2048,768]{1,0:T(8,128)(2,1)S(1)}, bf16[2048,768]{1,0:T(8,128)(2,1)}, u32[]{:S(2)}) copy-start(bf16[2048,768]{1,0:T(8,128)(2,1)} %param.17) | copy-start | bytes 9437188
  2490.6 150.5 %copy-start.25 = (f32[768]{0:T(1024)S(1)}, f32[768]{0:T(1024)}, u32[]{:S(2)}) copy-start(f32[768]{0:T(1024)} %get-tuple-element.165) | copy-start | bytes 9220
  2490.6 231.2 %all-gather.29.cloned.1.call-start = ((), (), s32[]{:S(2)}) async-start(), calls=%async_computation.8 | async-start | bytes 9437184 | tf_op jit(solution)/shard_map/all_gather | solution.py:92
  2643.4 819.5 %reduce-scatter.9.cloned.1.call-start = ((), (), s32[]{:S(2)}) async-start(), calls=%async_computation.9 | async-start | bytes 18874368 | tf_op jit(solution)/shard_map/reduce_scatter | solution.py:100
  2660.9 40.1 copy-start.14
  3320.3 582.3 %all-gather.43.cloned.1.call-start = ((), (), s32[]{:S(2)}) async-start(), calls=%async_computation.17 | async-start | bytes 94371840 | tf_op jit(solution)/shard_map/all_gather | solution.py:91
  3341.2 129.8 %copy-start.26 = (f32[768]{0:T(1024)S(1)}, f32[768]{0:T(1024)}, u32[]{:S(2)}) copy-start(f32[768]{0:T(1024)} %get-tuple-element.163) | copy-start | bytes 9220
  3341.2 653.9 %all-gather.31.cloned.1.call-start = ((), (), s32[]{:S(2)}) async-start(), calls=%async_computation.10 | async-start | bytes 9437184 | tf_op jit(solution)/shard_map/all_gather | solution.py:101
  3473.4 948.6 %all-gather.39.cloned.1.call-start = ((), (), s32[]{:S(2)}) async-start(), calls=%async_computation.15 | async-start | bytes 94371840 | tf_op jit(solution)/shard_map/all_gather | solution.py:89
  3474.0 1387.7 %all-gather.41.cloned.1.call-start = ((), (), s32[]{:S(2)}) async-start(), calls=%async_computation.16 | async-start | bytes 94371840 | tf_op jit(solution)/shard_map/all_gather | solution.py:90
  3474.7 520.4 %copy-start.22 = (s32[8192]{0:T(1024)S(1)}, s32[8192]{0:T(1024)}, u32[]{:S(2)}) copy-start(s32[8192]{0:T(1024)} %copy-done.21) | copy-start | bytes 98308
  3474.7 1815.0 %reduce-scatter.11.cloned.1.call-start = ((), (), s32[]{:S(2)}) async-start(), calls=%async_computation.11 | async-start | bytes 18874368 | tf_op jit(solution)/shard_map/reduce_scatter | solution.py:103
  4997.4 87.2 %copy-start.20 = (f32[8192]{0:T(1024)S(1)}, f32[8192]{0:T(1024)}, u32[]{:S(2)}) copy-start(f32[8192]{0:T(1024)} %gather_fusion.1) | copy-start | bytes 98308
  (23 other events, 182.2 us)
Sparse Core Ops, SparseCore 0:
  15.1 81.0 all-gather.24
  700.4 143.0 reduce-scatter.4
  850.5 78.2 all-gather.26
  930.1 438.1 all-gather.32
  1369.7 438.1 all-gather.34
  1809.3 438.3 all-gather.36
  2490.7 141.9 reduce-scatter.6
  2643.5 78.2 all-gather.28
  3320.4 142.3 reduce-scatter.8
  3464.2 438.3 all-gather.42
  3904.1 78.2 all-gather.30
  3983.8 438.1 all-gather.38
  4423.5 438.1 all-gather.40
  5148.1 141.6 reduce-scatter.10
where the time goes:
time: 5330 us; the launch traced here: 5300 us
  waiting for transfers between devices  2570 us (48%)
  matrix products  739 us (14%)
  other arithmetic  736 us (14%)
  Pallas kernels  558 us (10%)
  local copies, waits for them, and re-layouts  524 us (10%)
  blocking collectives  158 us (3%)
    all_gather x2, waiting for transfers between devices, device_step(): down_weight = lax.all_gather(w_down[layer], 'tok', axis=2, tiled=True)  732 us
    all_gather x2, waiting for transfers between devices, device_step(): up_weight = lax.all_gather(w_up[layer], 'tok', axis=1, tiled=True)  689 us
    all_gather x2, waiting for transfers between devices, device_step(): gate_weight = lax.all_gather(w_gate[layer], 'tok', axis=1, tiled=True)  604 us
    another operation x6, Pallas kernels  555 us
    reduce_sum x16, other arithmetic, one_block(): jax.nn.softmax(jnp.where(allowed, scores, -1e+30), axis=-1)  362 us
    dot_general x16, matrix products, one_block(): jnp.einsum('bhgd,shd->hgbs', q_block, k_rot, preferred_element_type=jnp.f...  350 us
    dot_general x16, matrix products, one_block(): jnp.einsum('hgbs,shd->bhgd', attn_prob, v_all, preferred_element_type=jnp...  348 us
    reduce_scatter x2, waiting for transfers between devices, device_step(): lax.psum_scatter(mix_part, 'mp', scatter_dimension=0, tiled=True)  284 us
  transfers between devices with their start and end apart: 14, of which 11 were waited for; matrix products, arithmetic and copies ran while one was open for 10% of the time, Pallas kernels for 5%

commit v1 on v0

v1 whole, which is shorter than its diff:
```python
import functools

import jax
import jax.numpy as jnp
from jax import lax
from jax.experimental import pallas as pl
from jax.experimental.pallas import tpu as pltpu
from jax.sharding import PartitionSpec as P

EPS = 1e-5
ROPE_BASE = 10000.0
NEG = -1e30
VMEM_LIMIT = 66_000_000
ROW_TILE = 288
CHUNKS = 2


def rms_norm(residual, gain):
    inv_rms = lax.rsqrt(jnp.mean(residual * residual, axis=-1, keepdims=True) + EPS)
    return (residual * inv_rms * gain.astype(jnp.float32)).astype(jnp.bfloat16)


def request_starts(seg_row):
    token_index = jnp.arange(seg_row.shape[0], dtype=jnp.int32)
    is_start = jnp.concatenate([jnp.ones((1,), dtype=jnp.bool_), seg_row[1:] != seg_row[:-1]])
    return lax.cummax(jnp.where(is_start, token_index, 0), axis=0)


def qkv_kernel(x_ref, w_ref, cos_ref, sin_ref, q_ref, k_ref, v_ref):
    width = q_ref.shape[1]
    reps = width // cos_ref.shape[1]
    cosines = jnp.concatenate([cos_ref[...]] * reps, axis=1)
    sines = jnp.concatenate([sin_ref[...]] * reps, axis=1)
    proj = jnp.dot(x_ref[...], w_ref[...], preferred_element_type=jnp.float32)
    q_ref[...] = ((proj[:, :width] * cosines + proj[:, width:2 * width] * sines) * 0.125).astype(jnp.bfloat16)
    k_ref[...] = (proj[:, 2 * width:3 * width] * cosines + proj[:, 3 * width:4 * width] * sines).astype(jnp.bfloat16)
    v_ref[...] = proj[:, 4 * width:].astype(jnp.bfloat16)


def project_qkv(normed, weight, cosines, sines):
    rows, hidden = normed.shape
    width = weight.shape[1] // 5
    block = 512
    row_block = pl.BlockSpec((block, width), lambda i: (i, 0))
    table = pl.BlockSpec((block, cosines.shape[1]), lambda i: (i, 0))
    return pl.pallas_call(
        qkv_kernel,
        grid=(rows // block,),
        in_specs=[pl.BlockSpec((block, hidden), lambda i: (i, 0)), pl.BlockSpec(weight.shape, lambda i: (0, 0)), table, table],
        out_specs=[row_block] * 3,
        out_shape=[jax.ShapeDtypeStruct((rows, width), jnp.bfloat16)] * 3,
        compiler_params=pltpu.CompilerParams(vmem_limit_bytes=VMEM_LIMIT),
        cost_estimate=pl.CostEstimate(flops=2 * rows * hidden * weight.shape[1], bytes_accessed=16 * 1024 * 1024, transcendentals=0),
        name="qkv",
    )(normed, weight, cosines, sines)


def attention_kernel(first_ref, q_ref, k_ref, v_ref, start_ref, o_ref):
    block = q_ref.shape[0]
    i = pl.program_id(1)
    q = q_ref[...]
    lane = lax.broadcasted_iota(jnp.int32, q.shape, 1)
    q_heads = [jnp.where(lane < 64, q, jnp.zeros_like(q)), jnp.where(lane < 64, jnp.zeros_like(q), q)]
    start = start_ref[...]
    row = i * block + lax.broadcasted_iota(jnp.int32, (block, block), 0)
    col = lax.broadcasted_iota(jnp.int32, (block, block), 1)

    def step(j, carry):
        keys = k_ref[pl.ds(pl.multiple_of(j * block, block), block), :]
        values = v_ref[pl.ds(pl.multiple_of(j * block, block), block), :]
        at = col + j * block
        allowed = (at >= start) & (at <= row)
        out = []
        for head in range(2):
            top, total, acc = carry[head]
            scores = lax.dot_general(q_heads[head], keys, (((1,), (1,)), ((), ())), preferred_element_type=jnp.float32)
            scores = jnp.where(allowed, scores, NEG)
            new_top = jnp.maximum(top, jnp.max(scores, axis=1, keepdims=True))
            prob = jnp.exp(scores - new_top)
            decay = jnp.exp(top - new_top)
            total = total * decay + jnp.sum(prob, axis=1, keepdims=True)
            acc = acc * decay + jnp.dot(prob.astype(jnp.bfloat16), values, preferred_element_type=jnp.float32)
            out.append((new_top, total, acc))
        return tuple(out)

    zero = (jnp.full((block, 1), NEG, jnp.float32), jnp.zeros((block, 1), jnp.float32), jnp.zeros(q.shape, jnp.float32))
    (_, total_a, acc_a), (_, total_b, acc_b) = lax.fori_loop(first_ref[i], i + 1, step, (zero, zero))
    o_ref[...] = jnp.where(lane < 64, acc_a / total_a, acc_b / total_b).astype(jnp.bfloat16)


def attention(q, k, v, starts):
    rows, width = q.shape
    block = 512
    first = starts[::block] // block
    grid_spec = pltpu.PrefetchScalarGridSpec(
        num_scalar_prefetch=1,
        grid=(width // 128, rows // block),
        in_specs=[
            pl.BlockSpec((block, 128), lambda p, i, f: (i, p)),
            pl.BlockSpec((rows, 128), lambda p, i, f: (0, p)),
            pl.BlockSpec((rows, 128), lambda p, i, f: (0, p)),
            pl.BlockSpec((block, 1), lambda p, i, f: (i, 0)),
        ],
        out_specs=pl.BlockSpec((block, 128), lambda p, i, f: (i, p)),
    )
    return pl.pallas_call(
        attention_kernel,
        grid_spec=grid_spec,
        out_shape=jax.ShapeDtypeStruct((rows, width), jnp.bfloat16),
        compiler_params=pltpu.CompilerParams(vmem_limit_bytes=VMEM_LIMIT),
        cost_estimate=pl.CostEstimate(flops=8 * rows * rows * width, bytes_accessed=16 * 1024 * 1024, transcendentals=rows * rows * 3),
        name="attention",
    )(first, q, k, v, starts[:, None])


def moe_kernel(tile_expert, tile_start, tile_count, place, token_ref, gate_ref, h_ref, g0, g1, g2, g3, u0, u1, u2, u3, d0, d1, d2, d3, out_ref, x_scr, y_scr, wg, wu, wd):
    i = pl.program_id(0)
    depth = g0.shape[1]

    @pl.when(i == 0)
    def _():
        out_ref[...] = jnp.zeros_like(out_ref)
        x_scr[...] = jnp.zeros_like(x_scr)

    @pl.when(i < place[1])
    def _():
        start, count = tile_start[i], tile_count[i]

        @pl.when((i == 0) | (tile_expert[i] != tile_expert[jnp.maximum(i - 1, 0)]))
        def _():
            for home in range(4):
                @pl.when(place[0] == home)
                def _():
                    for j, (g, u, d) in enumerate(((g0, u0, d0), (g1, u1, d1), (g2, u2, d2), (g3, u3, d3))):
                        at = (home ^ j) * depth
                        wg[at:at + depth, :] = g[0]
                        wu[at:at + depth, :] = u[0]
                        wd[:, at:at + depth] = d[0]

        def fetch(b, _):
            base = pl.multiple_of(b * 8, 8)
            rows = [h_ref[pl.ds(token_ref[start + base + r], 1), :] for r in range(8)]
            x_scr[pl.ds(base, 8), :] = jnp.concatenate(rows, axis=0)
            return 0

        lax.fori_loop(0, lax.div(count + 7, 8), fetch, 0)
        x = x_scr[...].astype(jnp.bfloat16)
        gate_pre = jnp.dot(x, wg[...], preferred_element_type=jnp.float32)
        up_pre = jnp.dot(x, wu[...], preferred_element_type=jnp.float32)
        act = (gate_pre * jax.nn.sigmoid(gate_pre) * up_pre).astype(jnp.bfloat16)
        y_scr[...] = jnp.dot(act, wd[...], preferred_element_type=jnp.float32)

        def add_eight(b, _):
            base = pl.multiple_of(b * 8, 8)
            part = y_scr[pl.ds(base, 8), :]
            tokens = [token_ref[start + base + r] for r in range(8)]
            sums = [out_ref[pl.ds(tokens[r], 1), :] + part[r:r + 1, :] * gate_ref[start + base + r] for r in range(8)]
            for r in range(8):
                out_ref[pl.ds(tokens[r], 1), :] = sums[r]
            return 0

        def add_one(r, _):
            token = token_ref[start + r]
            out_ref[pl.ds(token, 1), :] = out_ref[pl.ds(token, 1), :] + y_scr[pl.ds(r, 1), :] * gate_ref[start + r]
            return 0

        full = lax.div(count, 8)
        lax.fori_loop(0, full, add_eight, 0)
        lax.fori_loop(full * 8, count, add_one, 0)


def run_experts(h_rows, tables, place, tokens, gates, gate_parts, up_parts, down_parts):
    tile_expert, tile_start, tile_count, num_tiles = tables
    place = jnp.stack([place, num_tiles])
    rows, hidden = h_rows.shape
    _, depth, width = gate_parts[0].shape
    whole = lambda i, *_: (0, 0)
    pick = lambda i, te, *_: (te[i], 0, 0)
    grid_spec = pltpu.PrefetchScalarGridSpec(
        num_scalar_prefetch=6,
        grid=(tile_expert.shape[0],),
        in_specs=[pl.BlockSpec((rows, hidden), whole, pipeline_mode=pl.Buffered(1))]
        + [pl.BlockSpec((1, depth, width), pick)] * 8
        + [pl.BlockSpec((1, width, depth), pick)] * 4,
        out_specs=pl.BlockSpec((rows, hidden), whole, pipeline_mode=pl.Buffered(1)),
        scratch_shapes=[
            pltpu.VMEM((ROW_TILE, hidden), jnp.float32),
            pltpu.VMEM((ROW_TILE, hidden), jnp.float32),
            pltpu.VMEM((hidden, width), jnp.bfloat16),
            pltpu.VMEM((hidden, width), jnp.bfloat16),
            pltpu.VMEM((width, hidden), jnp.bfloat16),
        ],
    )
    experts = gate_parts[0].shape[0]
    return pl.pallas_call(
        moe_kernel,
        grid_spec=grid_spec,
        out_shape=jax.ShapeDtypeStruct((rows, hidden), jnp.float32),
        compiler_params=pltpu.CompilerParams(vmem_limit_bytes=VMEM_LIMIT),
        cost_estimate=pl.CostEstimate(flops=12 * 256 * experts * hidden * width, bytes_accessed=80 * 1024 * 1024, transcendentals=0),
        name="experts",
    )(tile_expert, tile_start, tile_count, place, tokens, gates, h_rows, *gate_parts, *up_parts, *down_parts)


def tile_tables(sizes, first_expert, experts, max_pairs):
    order = jnp.arange(sizes.shape[0], dtype=jnp.int32)
    offsets = jnp.sum(jnp.where(order[None, :] < order[:, None], sizes[None, :], 0), axis=1)
    count = lax.dynamic_slice_in_dim(sizes, first_expert, experts)
    offset = lax.dynamic_slice_in_dim(offsets, first_expert, experts)
    tiles = (count + ROW_TILE - 1) // ROW_TILE
    local = jnp.arange(experts, dtype=jnp.int32)
    first_tile = jnp.sum(jnp.where(local[None, :] < local[:, None], tiles[None, :], 0), axis=1)
    num_tiles = jnp.sum(tiles)
    last = jnp.max(jnp.where(tiles > 0, local, 0))
    max_tiles = (max_pairs - experts) // ROW_TILE + experts
    tile = jnp.arange(max_tiles, dtype=jnp.int32)
    mine = (tile[:, None] >= first_tile[None, :]) & (tile[:, None] < (first_tile + tiles)[None, :])
    pick = lambda values: jnp.sum(jnp.where(mine, values, 0), axis=1).astype(jnp.int32)
    done = (tile[:, None] - first_tile[None, :]) * ROW_TILE
    return jnp.where(tile < num_tiles, pick(local[None, :]), last), pick(offset[None, :] + done), pick(jnp.minimum(count[None, :] - done, ROW_TILE)), num_tiles.astype(jnp.int32)


def solution(mesh):
    token_spec = P(('rep', 'tok', 'mp'))
    row_spec = P(('rep', 'tok', 'mp'), None)
    head_weight = P(None, 'tok', 'mp', None)
    in_specs = (row_spec, token_spec, row_spec, row_spec, head_weight, head_weight, head_weight, P(None, 'mp', None, 'tok'), P(None, None, 'tok', 'mp'), P(None, None, 'tok', 'mp'), P(None, None, 'mp', 'tok'), P(None, None), P(None, None))

    def swap_mp(value):
        return lax.ppermute(value, 'mp', [(0, 1), (1, 0)])

    def swap_chip(value):
        return lax.ppermute(value, 'tok', [(i, i ^ 2) for i in range(4)])

    def swap_core(value):
        return lax.ppermute(value, 'tok', [(i, i ^ 1) for i in range(4)])

    def swap_diagonal(value):
        return lax.ppermute(value, ('mp', 'tok'), [(i, i ^ 6) for i in range(8)])

    def device_step(hidden_in, seg_ids, expert_ids, expert_gates, w_query, w_key, w_value, w_out, w_gate, w_up, w_down, gain_attn, gain_mlp):
        num_layers, depth, q_local, head_dim = w_query.shape
        num_experts = w_gate.shape[1]
        rows, hidden = hidden_in.shape
        half_experts = num_experts // 2
        chunk = half_experts // CHUNKS
        m = lax.axis_index('mp')
        t = lax.axis_index('tok')
        chip = t // 2
        place = t.astype(jnp.int32)

        def join(mine, other, axis=0):
            first = jnp.where(m == 0, mine, other)
            second = jnp.where(m == 0, other, mine)
            return jnp.concatenate([first, second], axis=axis)

        def gather_mp(value):
            return join(value, swap_mp(value))

        qkv_local = jnp.concatenate([w.reshape(num_layers, depth, q_local * head_dim) for w in (w_query, w_key, w_value)], axis=2)
        qkv_all = lax.all_gather(qkv_local, 'tok', axis=1, tiled=True)
        out_all = lax.all_gather(w_out.reshape(num_layers, q_local * head_dim, depth), ('mp', 'tok'), axis=0)
        out_all = out_all.reshape(2, 4, num_layers, q_local * head_dim, depth).transpose(2, 0, 3, 1, 4).reshape(num_layers, 2 * q_local * head_dim, hidden)

        def rotated(weight):
            parts = weight.reshape(hidden, q_local, 2, head_dim // 2)
            return jnp.concatenate([-parts[:, :, 1:], parts[:, :, :1]], axis=2).reshape(hidden, q_local * head_dim)

        seg_full = gather_mp(seg_ids)
        starts = request_starts(seg_full)
        seq_len = seg_full.shape[0]
        positions = jnp.arange(seq_len, dtype=jnp.int32) - starts
        inv_freq = jnp.power(ROPE_BASE, -jnp.arange(head_dim // 2, dtype=jnp.float32) * 2.0 / head_dim)
        angles = positions.astype(jnp.float32)[:, None] * inv_freq
        cosines = jnp.tile(jnp.cos(angles), (1, 4))
        sines = jnp.tile(jnp.sin(angles), (1, 4))

        flat_ids = gather_mp(expert_ids).reshape(2 * seq_len)
        flat_gates = gather_mp(expert_gates).reshape(2 * seq_len)
        pair_token = jnp.arange(2 * seq_len, dtype=jnp.int32) // 2
        _, tokens_own, gates_own = lax.sort((flat_ids, pair_token, flat_gates), num_keys=1)
        sizes_own = jnp.sum((flat_ids[:, None] == jnp.arange(num_experts, dtype=jnp.int32)[None, :]).astype(jnp.int32), axis=0)
        pad = jnp.zeros((8,), jnp.int32)
        ints_own = jnp.concatenate([sizes_own, tokens_own, pad])
        floats_own = jnp.concatenate([gates_own, pad.astype(jnp.float32)])
        ints_far = swap_chip(ints_own)
        floats_far = swap_chip(floats_own)
        routing = []
        for ints, floats in ((ints_far, floats_far), (ints_own, floats_own)):
            tables = [tile_tables(ints[:num_experts], chip * half_experts + c * chunk, chunk, 2 * seq_len) for c in range(CHUNKS)]
            routing.append((tables, ints[num_experts:], floats))

        def exchange(weight, layer, c):
            near = lax.dynamic_slice_in_dim(weight[layer], chip * half_experts + c * chunk, chunk, 0)
            far = lax.dynamic_slice_in_dim(weight[layer], (1 - chip) * half_experts + c * chunk, chunk, 0)
            return near, far

        def spread(near, far):
            crossed = swap_chip(far)
            return near, swap_core(near), crossed, swap_core(crossed)

        residual = hidden_in.astype(jnp.float32)
        for layer in range(num_layers):
            q_w, k_w, v_w = jnp.split(qkv_all[layer], 3, axis=1)
            weight = jnp.concatenate([q_w, rotated(q_w), k_w, rotated(k_w), v_w], axis=1)
            normed = gather_mp(rms_norm(residual, gain_attn[layer]))
            q, k, v = project_qkv(normed, weight, cosines, sines)
            attn = attention(q, k, v, starts)
            keep = lax.dynamic_slice_in_dim(attn, m * rows, rows, 0)
            send = lax.dynamic_slice_in_dim(attn, (1 - m) * rows, rows, 0)
            attn_full = join(keep, swap_mp(send), axis=1)
            residual = residual + jnp.dot(attn_full, out_all[layer], preferred_element_type=jnp.float32)
            normed = rms_norm(residual, gain_mlp[layer])
            far_half = swap_chip(normed)
            h_own = gather_mp(normed).astype(jnp.float32)
            h_far = gather_mp(far_half).astype(jnp.float32)
            parts = [None, None]
            for c in range(CHUNKS):
                gate_parts, up_parts, down_parts = [spread(*exchange(w, layer, c)) for w in (w_gate, w_up, w_down)]
                for s, h_rows in enumerate((h_far, h_own)):
                    tables, tokens, gates = routing[s]
                    got = run_experts(h_rows, tables[c], place, tokens, gates, gate_parts, up_parts, down_parts)
                    parts[s] = got if parts[s] is None else parts[s] + got
            far_sum, own_sum = parts
            pick = lambda value, which: lax.dynamic_slice_in_dim(value, which * rows, rows, 0)
            from_chip = swap_chip(pick(far_sum, m))
            from_diagonal = swap_diagonal(pick(far_sum, 1 - m))
            from_mp = swap_mp(pick(own_sum, 1 - m))
            residual = residual + pick(own_sum, m) + from_mp + from_chip + from_diagonal
        return residual

    return jax.shard_map(device_step, mesh=mesh, in_specs=in_specs, out_specs=row_spec, check_vma=False)
```

time: 5330 us -> 2930 us (0.55)
  waiting for transfers between devices: 2570 us -> 1530 us
  matrix products: 739 us -> 8.13 us
  other arithmetic: 736 us -> 175 us
  Pallas kernels: 558 us -> 756 us
  blocking collectives: 158 us -> 0 us
  local copies, waits for them, and re-layouts: 524 us -> 390 us
    all_gather x10 -> x2, waiting for transfers between devices: 2020 us -> 0.01 us  [the longest x1 0.01 us: device_step(): qkv_all = lax.all_gather(qkv_local, 'tok', axis=1, tiled=True)]
    ppermute x0 -> x57, waiting for transfers between devices: none -> 1530 us  [the longest x18 1050 us: swap_chip(): return lax.ppermute(value, 'tok', [(i, i ^ 2) for i in range(4)])]
    pallas_call x0 -> x12, Pallas kernels: none -> 756 us  [the longest x8 517 us: run_experts(): pl.pallas_call(moe_kernel, grid_spec=grid_spec, out_shape=jax.ShapeDtypeS...]
    dot_general x34 -> x2, matrix products: 719 us -> 8.13 us  [device_step(): jnp.dot(attn_full, out_all[layer], preferred_element_type=jnp.float32)]
    another operation x6 -> x0, Pallas kernels: 555 us -> none
    reduce_scatter x4 -> x0, waiting for transfers between devices: 547 us -> none  [the longest x2 284 us: device_step(): lax.psum_scatter(mix_part, 'mp', scatter_dimension=0, tiled=True)]
    reduce_sum x16 -> x11, other arithmetic: 362 us -> 4.86 us  [the longest x4 2.53 us: tile_tables(): jnp.sum(jnp.where(mine, values, 0), axis=1).astype(jnp.int32)]
    all_gather x12 -> x0, local copies, waits for them, and re-layouts: 197 us -> none  [the longest x2 185 us: device_step(): down_weight = lax.all_gather(w_down[layer], 'tok', axis=2, tiled=True)]
  transfers between devices with their start and end apart: 14 -> 59, of which waited for: 11 -> 18; matrix products, arithmetic and copies ran while one was open for 10% -> 18% of each run, Pallas kernels for 5% -> 26%
where the time goes in v1:
time: 2930 us; the launch traced here: 2920 us
  waiting for transfers between devices  1530 us (52%)
  Pallas kernels  756 us (26%)
  local copies, waits for them, and re-layouts  390 us (13%)
  other arithmetic  175 us (6%)
  starting transfers between devices  40.1 us (1%)
    ppermute x18, waiting for transfers between devices, swap_chip(): return lax.ppermute(value, 'tok', [(i, i ^ 2) for i in range(4)])  1050 us
    pallas_call x8, Pallas kernels, run_experts(): pl.pallas_call(moe_kernel, grid_spec=grid_spec, out_shape=jax.ShapeDtypeS...  517 us
    ppermute x2, waiting for transfers between devices, swap_diagonal(): return lax.ppermute(value, ('mp', 'tok'), [(i, i ^ 6) for i in range(8)])  273 us
    ppermute x13, waiting for transfers between devices, swap_mp(): return lax.ppermute(value, 'mp', [(0, 1), (1, 0)])  209 us
    pallas_call x2, Pallas kernels, attention(): pl.pallas_call(attention_kernel, grid_spec=grid_spec, out_shape=jax.Shape...  204 us
    slice x3, local copies, waits for them, and re-layouts, exchange(): weight[layer]  75.8 us
    dynamic_slice x6, local copies, waits for them, and re-layouts, exchange(): lax.dynamic_slice_in_dim(weight[layer], (1 - chip) * half_experts + c * c...  72 us
    ppermute x8, local copies, waits for them, and re-layouts, swap_core(): return lax.ppermute(value, 'tok', [(i, i ^ 1) for i in range(4)])  63.4 us
  transfers between devices with their start and end apart: 59, of which 18 were waited for; matrix products, arithmetic and copies ran while one was open for 18% of the time, Pallas kernels for 26%

profile of v1, /device:TPU:0, one launch (start us, length us, event | category | flops | bytes accessed | tf_op | source)
XLA Modules:
  0.0 2917.4 jit_solution(16872446974397961871)
XLA Ops:
  188.5 160.3 %collective-permute-done.25 = s32[8232]{0:T(1024)S(1)} collective-permute-done((s32[8232]{0:T(1024)S(1)}, s32[8232]{0:T(1024)S(1)}, u32[]{:S(2)}, u32[]{:S(2)}) %collective-permute-start.25) | collective-permute-done | bytes 32960 | tf_op jit(solution)/shard_map/ppermute | solution.py:233
  411.5 102.0 %attention.2 = bf16[4096,384]{1,0:T(8,128)(2,1)} custom-call(s32[8]{0:T(128)} %and_select_fusion.4.first_ref, bf16[4096,384]{1,0:T(8,128)(2,1)} %get-tuple-element.16.q_ref, bf16[4096,384]{1,0:T(8,128)(2,1)} %get-tuple-element.17.k_ref, bf16[4096,384]{1,0:T(8,128)(2,1)} %get-tuple-element.18.v_ref, s32[4096,1]{1,0:T(8,128)} %copy.175.start_ref), custom_call_target="tpu_custom_call" | custom-call | flops 51539607552 | bytes 16777216 | tf_op jit(solution)/shard_map/attention/pallas_call | solution.py:106
  557.4 55.8 %collective-permute-done.16.g2 = bf16[8,192,1536]{2,1,0:T(8,128)(2,1)} collective-permute-done((bf16[8,192,1536]{2,1,0:T(8,128)(2,1)}, bf16[8,192,1536]{2,1,0:T(8,128)(2,1)}, u32[]{:S(2)}, u32[]{:S(2)}) %collective-permute-start.16) | collective-permute-done | bytes 4718624 | tf_op jit(solution)/shard_map/ppermute | solution.py:233
  613.2 101.1 %collective-permute-done.19.u2 = bf16[8,192,1536]{2,1,0:T(8,128)(2,1)} collective-permute-done((bf16[8,192,1536]{2,1,0:T(8,128)(2,1)}, bf16[8,192,1536]{2,1,0:T(8,128)(2,1)}, u32[]{:S(2)}, u32[]{:S(2)}) %collective-permute-start.19) | collective-permute-done | bytes 4718624 | tf_op jit(solution)/shard_map/ppermute | solution.py:233
  714.3 100.1 %collective-permute-done.22 = bf16[8,1536,192]{1,2,0:T(8,128)(2,1)} collective-permute-done((bf16[8,1536,192]{1,2,0:T(8,128)(2,1)}, bf16[8,1536,192]{1,2,0:T(8,128)(2,1)}, u32[]{:S(2)}, u32[]{:S(2)}) %collective-permute-start.22) | collective-permute-done | bytes 4718624 | tf_op jit(solution)/shard_map/ppermute | solution.py:233
  852.4 38.2 %collective-permute-done.5 = bf16[2048,768]{1,0:T(8,128)(2,1)} collective-permute-done((bf16[2048,768]{1,0:T(8,128)(2,1)S(1)}, bf16[2048,768]{1,0:T(8,128)(2,1)}, u32[]{:S(2)}, u32[]{:S(2)}) %collective-permute-start.5) | collective-permute-done | bytes 3145760 | tf_op jit(solution)/shard_map/ppermute | solution.py:230
  955.0 67.5 %experts.8 = f32[4096,768]{1,0:T(8,128)} custom-call(s32[36]{0:T(128)} %compare_select_fusion.7.tile_expert, s32[36]{0:T(128)} %get-tuple-element.32.tile_start, s32[36]{0:T(128)} %get-tuple-element.31.tile_count, s32[2]{0:T(128)} %get-tuple-element.156.place, s32[8200]{0:T(1024)} %concatenate.79.token_ref, f32[8200]{0:T(1024)} %concatenate.80.gate_ref, ...), custom_call_target="tpu_custom_call" | custom-call | flops 28991029248 | bytes 83886080 | tf_op jit(solution)/shard_map/experts/pallas_call | solution.py:195
  1022.6 63.4 %experts.9 = f32[4096,768]{1,0:T(8,128)} custom-call(s32[36]{0:T(128)} %compare_select_fusion.5.tile_expert, s32[36]{0:T(128)} %get-tuple-element.29.tile_start, s32[36]{0:T(128)} %get-tuple-element.28.tile_count, s32[2]{0:T(128)} %get-tuple-element.157.place, s32[8200]{0:T(1024)} %concatenate.79.token_ref, f32[8200]{0:T(1024)} %concatenate.80.gate_ref, ...), custom_call_target="tpu_custom_call" | custom-call | flops 28991029248 | bytes 83886080 | tf_op jit(solution)/shard_map/experts/pallas_call | solution.py:195
  1111.5 63.6 %experts.10 = f32[4096,768]{1,0:T(8,128)} custom-call(s32[36]{0:T(128)} %compare_select_fusion.3.tile_expert, s32[36]{0:T(128)} %get-tuple-element.38.tile_start, s32[36]{0:T(128)} %get-tuple-element.37.tile_count, s32[2]{0:T(128)} %get-tuple-element.158.place, s32[8200]{0:T(1024)} %slice.152.token_ref, f32[8200]{0:T(1024)} %copy-done.25, ...), custom_call_target="tpu_custom_call" | custom-call | flops 28991029248 | bytes 83886080 | tf_op jit(solution)/shard_map/experts/pallas_call | solution.py:195
  1175.1 64.1 %experts.11 = f32[4096,768]{1,0:T(8,128)} custom-call(s32[36]{0:T(128)} %compare_select_fusion.1.tile_expert, s32[36]{0:T(128)} %get-tuple-element.35.tile_start, s32[36]{0:T(128)} %get-tuple-element.34.tile_count, s32[2]{0:T(128)} %get-tuple-element.159.place, s32[8200]{0:T(1024)} %slice.152.token_ref, f32[8200]{0:T(1024)} %copy-done.25, ...), custom_call_target="tpu_custom_call" | custom-call | flops 28991029248 | bytes 83886080 | tf_op jit(solution)/shard_map/experts/pallas_call | solution.py:195
  1266.7 136.4 %collective-permute-done.30 = f32[2048,768]{1,0:T(8,128)S(1)} collective-permute-done((f32[2048,768]{1,0:T(8,128)}, f32[2048,768]{1,0:T(8,128)S(1)}, u32[]{:S(2)}, u32[]{:S(2)}) %collective-permute-start.30) | collective-permute-done | bytes 6291488 | tf_op jit(solution)/shard_map/ppermute | solution.py:239
  1405.7 127.3 %collective-permute-done.29 = f32[2048,768]{1,0:T(8,128)} collective-permute-done((f32[2048,768]{1,0:T(8,128)S(1)}, f32[2048,768]{1,0:T(8,128)}, u32[]{:S(2)}, u32[]{:S(2)}) %collective-permute-start.29) | collective-permute-done | bytes 6291488 | tf_op jit(solution)/shard_map/ppermute | solution.py:233
  1667.5 99.1 %collective-permute-done.38.u2 = bf16[8,192,1536]{2,1,0:T(8,128)(2,1)} collective-permute-done((bf16[8,192,1536]{2,1,0:T(8,128)(2,1)}, bf16[8,192,1536]{2,1,0:T(8,128)(2,1)}, u32[]{:S(2)}, u32[]{:S(2)}) %collective-permute-start.38) | collective-permute-done | bytes 4718624 | tf_op jit(solution)/shard_map/ppermute | solution.py:233
  1767.7 101.6 %attention.3 = bf16[4096,384]{1,0:T(8,128)(2,1)} custom-call(s32[8]{0:T(128)} %and_select_fusion.4.first_ref, bf16[4096,384]{1,0:T(8,128)(2,1)} %get-tuple-element.21.q_ref, bf16[4096,384]{1,0:T(8,128)(2,1)} %get-tuple-element.22.k_ref, bf16[4096,384]{1,0:T(8,128)(2,1)} %get-tuple-element.23.v_ref, s32[4096,1]{1,0:T(8,128)} %copy.175.start_ref), custom_call_target="tpu_custom_call" | custom-call | flops 51539607552 | bytes 16777216 | tf_op jit(solution)/shard_map/attention/pallas_call | solution.py:106
  1910.7 58.1 %collective-permute-done.44.g2 = bf16[8,192,1536]{2,1,0:T(8,128)(2,1)} collective-permute-done((bf16[8,192,1536]{2,1,0:T(8,128)(2,1)}, bf16[8,192,1536]{2,1,0:T(8,128)(2,1)}, u32[]{:S(2)}, u32[]{:S(2)}) %collective-permute-start.44) | collective-permute-done | bytes 4718624 | tf_op jit(solution)/shard_map/ppermute | solution.py:233
  1968.8 101.1 %collective-permute-done.47.u2 = bf16[8,192,1536]{2,1,0:T(8,128)(2,1)} collective-permute-done((bf16[8,192,1536]{2,1,0:T(8,128)(2,1)}, bf16[8,192,1536]{2,1,0:T(8,128)(2,1)}, u32[]{:S(2)}, u32[]{:S(2)}) %collective-permute-start.47) | collective-permute-done | bytes 4718624 | tf_op jit(solution)/shard_map/ppermute | solution.py:233
  2070.0 100.7 %collective-permute-done.50 = bf16[8,1536,192]{1,2,0:T(8,128)(2,1)} collective-permute-done((bf16[8,1536,192]{1,2,0:T(8,128)(2,1)}, bf16[8,1536,192]{1,2,0:T(8,128)(2,1)}, u32[]{:S(2)}, u32[]{:S(2)}) %collective-permute-start.50) | collective-permute-done | bytes 4718624 | tf_op jit(solution)/shard_map/ppermute | solution.py:233
  2180.8 68.0 %collective-permute-done.33 = bf16[2048,768]{1,0:T(8,128)(2,1)S(1)} collective-permute-done((bf16[2048,768]{1,0:T(8,128)(2,1)S(1)}, bf16[2048,768]{1,0:T(8,128)(2,1)S(1)}, u32[]{:S(2)}, u32[]{:S(2)}) %collective-permute-start.33) | collective-permute-done | bytes 3145760 | tf_op jit(solution)/shard_map/ppermute | solution.py:230
  2324.7 67.1 %experts.12 = f32[4096,768]{1,0:T(8,128)} custom-call(s32[36]{0:T(128)} %compare_select_fusion.7.tile_expert, s32[36]{0:T(128)} %get-tuple-element.32.tile_start, s32[36]{0:T(128)} %get-tuple-element.31.tile_count, s32[2]{0:T(128)} %get-tuple-element.156.place, s32[8200]{0:T(1024)} %concatenate.79.token_ref, f32[8200]{0:T(1024)} %concatenate.80.gate_ref, ...), custom_call_target="tpu_custom_call" | custom-call | flops 28991029248 | bytes 83886080 | tf_op jit(solution)/shard_map/experts/pallas_call | solution.py:195
  2391.8 63.4 %experts.13 = f32[4096,768]{1,0:T(8,128)} custom-call(s32[36]{0:T(128)} %compare_select_fusion.5.tile_expert, s32[36]{0:T(128)} %get-tuple-element.29.tile_start, s32[36]{0:T(128)} %get-tuple-element.28.tile_count, s32[2]{0:T(128)} %get-tuple-element.157.place, s32[8200]{0:T(1024)} %concatenate.79.token_ref, f32[8200]{0:T(1024)} %concatenate.80.gate_ref, ...), custom_call_target="tpu_custom_call" | custom-call | flops 28991029248 | bytes 83886080 | tf_op jit(solution)/shard_map/experts/pallas_call | solution.py:195
  2480.9 63.6 %experts.14 = f32[4096,768]{1,0:T(8,128)} custom-call(s32[36]{0:T(128)} %compare_select_fusion.3.tile_expert, s32[36]{0:T(128)} %get-tuple-element.38.tile_start, s32[36]{0:T(128)} %get-tuple-element.37.tile_count, s32[2]{0:T(128)} %get-tuple-element.158.place, s32[8200]{0:T(1024)} %slice.152.token_ref, f32[8200]{0:T(1024)} %copy-done.25, ...), custom_call_target="tpu_custom_call" | custom-call | flops 28991029248 | bytes 83886080 | tf_op jit(solution)/shard_map/experts/pallas_call | solution.py:195
  2544.5 64.1 %experts.15 = f32[4096,768]{1,0:T(8,128)} custom-call(s32[36]{0:T(128)} %compare_select_fusion.1.tile_expert, s32[36]{0:T(128)} %get-tuple-element.35.tile_start, s32[36]{0:T(128)} %get-tuple-element.34.tile_count, s32[2]{0:T(128)} %get-tuple-element.159.place, s32[8200]{0:T(1024)} %slice.152.token_ref, f32[8200]{0:T(1024)} %copy-done.25, ...), custom_call_target="tpu_custom_call" | custom-call | flops 28991029248 | bytes 83886080 | tf_op jit(solution)/shard_map/experts/pallas_call | solution.py:195
  2633.1 137.0 %collective-permute-done.56 = f32[2048,768]{1,0:T(8,128)S(1)} collective-permute-done((f32[2048,768]{1,0:T(8,128)}, f32[2048,768]{1,0:T(8,128)S(1)}, u32[]{:S(2)}, u32[]{:S(2)}) %collective-permute-start.56) | collective-permute-done | bytes 6291488 | tf_op jit(solution)/shard_map/ppermute | solution.py:239
  2770.1 130.1 %collective-permute-done.55 = f32[2048,768]{1,0:T(8,128)S(1)} collective-permute-done((f32[2048,768]{1,0:T(8,128)S(1)}, f32[2048,768]{1,0:T(8,128)S(1)}, u32[]{:S(2)}, u32[]{:S(2)}) %collective-permute-start.55) | collective-permute-done | bytes 6291488 | tf_op jit(solution)/shard_map/ppermute | solution.py:233
  (344 shorter events, 769.7 us)
Async XLA Ops:
  6.5 342.9 %all-gather.3.cloned.1.call-start = ((), (), s32[]{:S(2)}) async-start(), calls=%async_computation | async-start | bytes 4423680 | tf_op jit(solution)/shard_map/all_gather | solution.py:261
  13.7 538.5 %all-gather.5.cloned.1.call-start = ((), (), s32[]{:S(2)}) async-start(), calls=%async_computation.1 | async-start | bytes 2654208 | tf_op jit(solution)/shard_map/all_gather | solution.py:262
  62.5 344.9 %collective-permute-start.6 = (bf16[8,192,1536]{2,1,0:T(8,128)(2,1)}, bf16[8,192,1536]{2,1,0:T(8,128)(2,1)}, u32[]{:S(2)}, u32[]{:S(2)}) collective-permute-start(bf16[8,192,1536]{2,1,0:T(8,128)(2,1)} %get-tuple-element.89.g0), channel_id=1, source_target_pairs={{0,1},{1,0},{2,3},{3,2},{4,5},{5,4},{6,7},{7,6}} | collective-permute-start | bytes 14155784 | tf_op jit(solution)/shard_map/ppermute | solution.py:236
  142.5 266.6 %collective-permute-start.7 = (bf16[8,192,1536]{2,1,0:T(8,128)(2,1)}, bf16[8,192,1536]{2,1,0:T(8,128)(2,1)}, u32[]{:S(2)}, u32[]{:S(2)}) collective-permute-start(bf16[8,192,1536]{2,1,0:T(8,128)(2,1)} %get-tuple-element.88), channel_id=1, source_target_pairs={{0,2},{1,3},{2,0},{3,1},{4,6},{5,7},{6,4},{7,5}} | collective-permute-start | bytes 14155784 | tf_op jit(solution)/shard_map/ppermute | solution.py:233
  161.7 247.7 %collective-permute-start.9 = (bf16[8,192,1536]{2,1,0:T(8,128)(2,1)}, bf16[8,192,1536]{2,1,0:T(8,128)(2,1)}, u32[]{:S(2)}, u32[]{:S(2)}) collective-permute-start(bf16[8,192,1536]{2,1,0:T(8,128)(2,1)} %get-tuple-element.85.u0), channel_id=1, source_target_pairs={{0,1},{1,0},{2,3},{3,2},{4,5},{5,4},{6,7},{7,6}} | collective-permute-start | bytes 14155784 | tf_op jit(solution)/shard_map/ppermute | solution.py:236
  167.4 243.8 %collective-permute-start.10 = (bf16[8,192,1536]{2,1,0:T(8,128)(2,1)}, bf16[8,192,1536]{2,1,0:T(8,128)(2,1)}, u32[]{:S(2)}, u32[]{:S(2)}) collective-permute-start(bf16[8,192,1536]{2,1,0:T(8,128)(2,1)} %get-tuple-element.84), channel_id=1, source_target_pairs={{0,2},{1,3},{2,0},{3,1},{4,6},{5,7},{6,4},{7,5}} | collective-permute-start | bytes 14155784 | tf_op jit(solution)/shard_map/ppermute | solution.py:233
  409.1 204.1 %collective-permute-start.16 = (bf16[8,192,1536]{2,1,0:T(8,128)(2,1)}, bf16[8,192,1536]{2,1,0:T(8,128)(2,1)}, u32[]{:S(2)}, u32[]{:S(2)}) collective-permute-start(bf16[8,192,1536]{2,1,0:T(8,128)(2,1)} %get-tuple-element.86), channel_id=1, source_target_pairs={{0,2},{1,3},{2,0},{3,1},{4,6},{5,7},{6,4},{7,5}} | collective-permute-start | bytes 14155784 | tf_op jit(solution)/shard_map/ppermute | solution.py:233
  409.4 304.9 %collective-permute-start.19 = (bf16[8,192,1536]{2,1,0:T(8,128)(2,1)}, bf16[8,192,1536]{2,1,0:T(8,128)(2,1)}, u32[]{:S(2)}, u32[]{:S(2)}) collective-permute-start(bf16[8,192,1536]{2,1,0:T(8,128)(2,1)} %get-tuple-element.82), channel_id=1, source_target_pairs={{0,2},{1,3},{2,0},{3,1},{4,6},{5,7},{6,4},{7,5}} | collective-permute-start | bytes 14155784 | tf_op jit(solution)/shard_map/ppermute | solution.py:233
  411.2 408.9 %collective-permute-start.21 = (bf16[8,1536,192]{1,2,0:T(8,128)(2,1)}, bf16[8,1536,192]{1,2,0:T(8,128)(2,1)}, u32[]{:S(2)}, u32[]{:S(2)}) collective-permute-start(bf16[8,1536,192]{1,2,0:T(8,128)(2,1)} %bitcast.99), channel_id=1, source_target_pairs={{0,1},{1,0},{2,3},{3,2},{4,5},{5,4},{6,7},{7,6}} | collective-permute-start | bytes 14155784 | tf_op jit(solution)/shard_map/ppermute | solution.py:236
  411.2 403.2 %collective-permute-start.22 = (bf16[8,1536,192]{1,2,0:T(8,128)(2,1)}, bf16[8,1536,192]{1,2,0:T(8,128)(2,1)}, u32[]{:S(2)}, u32[]{:S(2)}) collective-permute-start(bf16[8,1536,192]{1,2,0:T(8,128)(2,1)} %get-tuple-element.78), channel_id=1, source_target_pairs={{0,2},{1,3},{2,0},{3,1},{4,6},{5,7},{6,4},{7,5}} | collective-permute-start | bytes 14155784 | tf_op jit(solution)/shard_map/ppermute | solution.py:233
  551.6 291.5 %collective-permute-start.8 = (bf16[8,192,1536]{2,1,0:T(8,128)(2,1)}, bf16[8,192,1536]{2,1,0:T(8,128)(2,1)}, u32[]{:S(2)}, u32[]{:S(2)}) collective-permute-start(bf16[8,192,1536]{2,1,0:T(8,128)(2,1)} %collective-permute-done.7.g2), channel_id=1, source_target_pairs={{0,1},{1,0},{2,3},{3,2},{4,5},{5,4},{6,7},{7,6}} | collective-permute-start | bytes 14155784 | tf_op jit(solution)/shard_map/ppermute | solution.py:236
  613.2 238.7 %collective-permute-start.11 = (bf16[8,192,1536]{2,1,0:T(8,128)(2,1)}, bf16[8,192,1536]{2,1,0:T(8,128)(2,1)}, u32[]{:S(2)}, u32[]{:S(2)}) collective-permute-start(bf16[8,192,1536]{2,1,0:T(8,128)(2,1)} %collective-permute-done.10.u2), channel_id=1, source_target_pairs={{0,1},{1,0},{2,3},{3,2},{4,5},{5,4},{6,7},{7,6}} | collective-permute-start | bytes 14155784 | tf_op jit(solution)/shard_map/ppermute | solution.py:236
  1266.7 266.3 %collective-permute-start.29 = (f32[2048,768]{1,0:T(8,128)S(1)}, f32[2048,768]{1,0:T(8,128)}, u32[]{:S(2)}, u32[]{:S(2)}) collective-permute-start(f32[2048,768]{1,0:T(8,128)S(1)} %get-tuple-element.92), channel_id=1, source_target_pairs={{0,2},{1,3},{2,0},{3,1},{4,6},{5,7},{6,4},{7,5}} | collective-permute-start | bytes 18874376 | tf_op jit(solution)/shard_map/ppermute | solution.py:233
  1647.9 223.1 %collective-permute-start.41 = (bf16[8,1536,192]{1,2,0:T(8,128)(2,1)}, bf16[8,1536,192]{1,2,0:T(8,128)(2,1)}, u32[]{:S(2)}, u32[]{:S(2)}) collective-permute-start(bf16[8,1536,192]{1,2,0:T(8,128)(2,1)} %get-tuple-element.68), channel_id=1, source_target_pairs={{0,2},{1,3},{2,0},{3,1},{4,6},{5,7},{6,4},{7,5}} | collective-permute-start | bytes 14155784 | tf_op jit(solution)/shard_map/ppermute | solution.py:233
  1665.5 303.4 %collective-permute-start.44 = (bf16[8,192,1536]{2,1,0:T(8,128)(2,1)}, bf16[8,192,1536]{2,1,0:T(8,128)(2,1)}, u32[]{:S(2)}, u32[]{:S(2)}) collective-permute-start(bf16[8,192,1536]{2,1,0:T(8,128)(2,1)} %get-tuple-element.74), channel_id=1, source_target_pairs={{0,2},{1,3},{2,0},{3,1},{4,6},{5,7},{6,4},{7,5}} | collective-permute-start | bytes 14155784 | tf_op jit(solution)/shard_map/ppermute | solution.py:233
  1666.6 403.3 %collective-permute-start.47 = (bf16[8,192,1536]{2,1,0:T(8,128)(2,1)}, bf16[8,192,1536]{2,1,0:T(8,128)(2,1)}, u32[]{:S(2)}, u32[]{:S(2)}) collective-permute-start(bf16[8,192,1536]{2,1,0:T(8,128)(2,1)} %get-tuple-element.70), channel_id=1, source_target_pairs={{0,2},{1,3},{2,0},{3,1},{4,6},{5,7},{6,4},{7,5}} | collective-permute-start | bytes 14155784 | tf_op jit(solution)/shard_map/ppermute | solution.py:233
  1766.6 411.6 %collective-permute-start.49 = (bf16[8,1536,192]{1,2,0:T(8,128)(2,1)}, bf16[8,1536,192]{1,2,0:T(8,128)(2,1)}, u32[]{:S(2)}, u32[]{:S(2)}) collective-permute-start(bf16[8,1536,192]{1,2,0:T(8,128)(2,1)} %bitcast.101), channel_id=1, source_target_pairs={{0,1},{1,0},{2,3},{3,2},{4,5},{5,4},{6,7},{7,6}} | collective-permute-start | bytes 14155784 | tf_op jit(solution)/shard_map/ppermute | solution.py:236
  1766.6 404.0 %collective-permute-start.50 = (bf16[8,1536,192]{1,2,0:T(8,128)(2,1)}, bf16[8,1536,192]{1,2,0:T(8,128)(2,1)}, u32[]{:S(2)}, u32[]{:S(2)}) collective-permute-start(bf16[8,1536,192]{1,2,0:T(8,128)(2,1)} %get-tuple-element.66), channel_id=1, source_target_pairs={{0,2},{1,3},{2,0},{3,1},{4,6},{5,7},{6,4},{7,5}} | collective-permute-start | bytes 14155784 | tf_op jit(solution)/shard_map/ppermute | solution.py:233
  1907.4 271.7 %collective-permute-start.36 = (bf16[8,192,1536]{2,1,0:T(8,128)(2,1)}, bf16[8,192,1536]{2,1,0:T(8,128)(2,1)S(1)}, u32[]{:S(2)}, u32[]{:S(2)}) collective-permute-start(bf16[8,192,1536]{2,1,0:T(8,128)(2,1)} %collective-permute-done.35.g2), channel_id=1, source_target_pairs={{0,1},{1,0},{2,3},{3,2},{4,5},{5,4},{6,7},{7,6}} | collective-permute-start | bytes 14155784 | tf_op jit(solution)/shard_map/ppermute | solution.py:236
  1968.8 211.4 %collective-permute-start.39 = (bf16[8,192,1536]{2,1,0:T(8,128)(2,1)}, bf16[8,192,1536]{2,1,0:T(8,128)(2,1)S(1)}, u32[]{:S(2)}, u32[]{:S(2)}) collective-permute-start(bf16[8,192,1536]{2,1,0:T(8,128)(2,1)} %collective-permute-done.38.u2), channel_id=1, source_target_pairs={{0,1},{1,0},{2,3},{3,2},{4,5},{5,4},{6,7},{7,6}} | collective-permute-start | bytes 14155784 | tf_op jit(solution)/shard_map/ppermute | solution.py:236
  2180.2 211.6 %collective-permute-start.43 = (bf16[8,192,1536]{2,1,0:T(8,128)(2,1)}, bf16[8,192,1536]{2,1,0:T(8,128)(2,1)}, u32[]{:S(2)}, u32[]{:S(2)}) collective-permute-start(bf16[8,192,1536]{2,1,0:T(8,128)(2,1)} %get-tuple-element.75.g0), channel_id=1, source_target_pairs={{0,1},{1,0},{2,3},{3,2},{4,5},{5,4},{6,7},{7,6}} | collective-permute-start | bytes 14155784 | tf_op jit(solution)/shard_map/ppermute | solution.py:236
  2180.2 211.5 %collective-permute-start.46 = (bf16[8,192,1536]{2,1,0:T(8,128)(2,1)}, bf16[8,192,1536]{2,1,0:T(8,128)(2,1)}, u32[]{:S(2)}, u32[]{:S(2)}) collective-permute-start(bf16[8,192,1536]{2,1,0:T(8,128)(2,1)} %get-tuple-element.71.u0), channel_id=1, source_target_pairs={{0,1},{1,0},{2,3},{3,2},{4,5},{5,4},{6,7},{7,6}} | collective-permute-start | bytes 14155784 | tf_op jit(solution)/shard_map/ppermute | solution.py:236
  2180.7 211.1 %collective-permute-start.45 = (bf16[8,192,1536]{2,1,0:T(8,128)(2,1)}, bf16[8,192,1536]{2,1,0:T(8,128)(2,1)}, u32[]{:S(2)}, u32[]{:S(2)}) collective-permute-start(bf16[8,192,1536]{2,1,0:T(8,128)(2,1)} %collective-permute-done.44.g2), channel_id=1, source_target_pairs={{0,1},{1,0},{2,3},{3,2},{4,5},{5,4},{6,7},{7,6}} | collective-permute-start | bytes 14155784 | tf_op jit(solution)/shard_map/ppermute | solution.py:236
  2630.8 269.4 %collective-permute-start.55 = (f32[2048,768]{1,0:T(8,128)S(1)}, f32[2048,768]{1,0:T(8,128)S(1)}, u32[]{:S(2)}, u32[]{:S(2)}) collective-permute-start(f32[2048,768]{1,0:T(8,128)S(1)} %get-tuple-element.90), channel_id=1, source_target_pairs={{0,2},{1,3},{2,0},{3,1},{4,6},{5,7},{6,4},{7,5}} | collective-permute-start | bytes 18874376 | tf_op jit(solution)/shard_map/ppermute | solution.py:233
  (73 other events, 5469.7 us)
Sparse Core Ops, SparseCore 0:
  13.8 30.5 all-gather.2
  63.6 34.8 all-gather.4

commit v2 on v1

--- a/solution.py
+++ b/solution.py
@@ -1,11 +1,10 @@
-import functools
-
 import jax
 import jax.numpy as jnp
 from jax import lax
 from jax.experimental import pallas as pl
 from jax.experimental.pallas import tpu as pltpu
 from jax.sharding import PartitionSpec as P
+
 
 EPS = 1e-5
 ROPE_BASE = 10000.0
@@ -50,7 +49,6 @@
         out_specs=[row_block] * 3,
         out_shape=[jax.ShapeDtypeStruct((rows, width), jnp.bfloat16)] * 3,
         compiler_params=pltpu.CompilerParams(vmem_limit_bytes=VMEM_LIMIT),
-        cost_estimate=pl.CostEstimate(flops=2 * rows * hidden * weight.shape[1], bytes_accessed=16 * 1024 * 1024, transcendentals=0),
         name="qkv",
     )(normed, weight, cosines, sines)
 
@@ -108,7 +106,6 @@
         grid_spec=grid_spec,
         out_shape=jax.ShapeDtypeStruct((rows, width), jnp.bfloat16),
         compiler_params=pltpu.CompilerParams(vmem_limit_bytes=VMEM_LIMIT),
-        cost_estimate=pl.CostEstimate(flops=8 * rows * rows * width, bytes_accessed=16 * 1024 * 1024, transcendentals=rows * rows * 3),
         name="attention",
     )(first, q, k, v, starts[:, None])
 
@@ -128,14 +125,11 @@
 
         @pl.when((i == 0) | (tile_expert[i] != tile_expert[jnp.maximum(i - 1, 0)]))
         def _():
-            for home in range(4):
-                @pl.when(place[0] == home)
-                def _():
-                    for j, (g, u, d) in enumerate(((g0, u0, d0), (g1, u1, d1), (g2, u2, d2), (g3, u3, d3))):
-                        at = (home ^ j) * depth
-                        wg[at:at + depth, :] = g[0]
-                        wu[at:at + depth, :] = u[0]
-                        wd[:, at:at + depth] = d[0]
+            for j, (g, u, d) in enumerate(((g0, u0, d0), (g1, u1, d1), (g2, u2, d2), (g3, u3, d3))):
+                at = pl.multiple_of((place[0] ^ j) * depth, depth)
+                wg[pl.ds(at, depth), :] = g[0]
+                wu[pl.ds(at, depth), :] = u[0]
+                wd[pl.ds(at, depth), :] = d[0]
 
         def fetch(b, _):
             base = pl.multiple_of(b * 8, 8)
@@ -148,7 +142,7 @@
         gate_pre = jnp.dot(x, wg[...], preferred_element_type=jnp.float32)
         up_pre = jnp.dot(x, wu[...], preferred_element_type=jnp.float32)
         act = (gate_pre * jax.nn.sigmoid(gate_pre) * up_pre).astype(jnp.bfloat16)
-        y_scr[...] = jnp.dot(act, wd[...], preferred_element_type=jnp.float32)
+        y_scr[...] = lax.dot_general(act, wd[...], (((1,), (1,)), ((), ())), preferred_element_type=jnp.float32)
 
         def add_eight(b, _):
             base = pl.multiple_of(b * 8, 8)
@@ -180,24 +174,21 @@
         num_scalar_prefetch=6,
         grid=(tile_expert.shape[0],),
         in_specs=[pl.BlockSpec((rows, hidden), whole, pipeline_mode=pl.Buffered(1))]
-        + [pl.BlockSpec((1, depth, width), pick)] * 8
-        + [pl.BlockSpec((1, width, depth), pick)] * 4,
+        + [pl.BlockSpec((1, depth, width), pick)] * 12,
         out_specs=pl.BlockSpec((rows, hidden), whole, pipeline_mode=pl.Buffered(1)),
         scratch_shapes=[
             pltpu.VMEM((ROW_TILE, hidden), jnp.float32),
             pltpu.VMEM((ROW_TILE, hidden), jnp.float32),
             pltpu.VMEM((hidden, width), jnp.bfloat16),
             pltpu.VMEM((hidden, width), jnp.bfloat16),
-            pltpu.VMEM((width, hidden), jnp.bfloat16),
+            pltpu.VMEM((hidden, width), jnp.bfloat16),
         ],
     )
-    experts = gate_parts[0].shape[0]
     return pl.pallas_call(
         moe_kernel,
         grid_spec=grid_spec,
         out_shape=jax.ShapeDtypeStruct((rows, hidden), jnp.float32),
         compiler_params=pltpu.CompilerParams(vmem_limit_bytes=VMEM_LIMIT),
-        cost_estimate=pl.CostEstimate(flops=12 * 256 * experts * hidden * width, bytes_accessed=80 * 1024 * 1024, transcendentals=0),
         name="experts",
     )(tile_expert, tile_start, tile_count, place, tokens, gates, h_rows, *gate_parts, *up_parts, *down_parts)
 
@@ -235,10 +226,7 @@
     def swap_core(value):
         return lax.ppermute(value, 'tok', [(i, i ^ 1) for i in range(4)])
 
-    def swap_diagonal(value):
-        return lax.ppermute(value, ('mp', 'tok'), [(i, i ^ 6) for i in range(8)])
-
-    def device_step(hidden_in, seg_ids, expert_ids, expert_gates, w_query, w_key, w_value, w_out, w_gate, w_up, w_down, gain_attn, gain_mlp):
+    def layers(hidden_in, seg_ids, expert_ids, expert_gates, w_query, w_key, w_value, w_out, w_gate, w_up, w_down, gain_attn, gain_mlp):
         num_layers, depth, q_local, head_dim = w_query.shape
         num_experts = w_gate.shape[1]
         rows, hidden = hidden_in.shape
@@ -290,15 +278,25 @@
             tables = [tile_tables(ints[:num_experts], chip * half_experts + c * chunk, chunk, 2 * seq_len) for c in range(CHUNKS)]
             routing.append((tables, ints[num_experts:], floats))
 
-        def exchange(weight, layer, c):
-            near = lax.dynamic_slice_in_dim(weight[layer], chip * half_experts + c * chunk, chunk, 0)
-            far = lax.dynamic_slice_in_dim(weight[layer], (1 - chip) * half_experts + c * chunk, chunk, 0)
-            return near, far
-
-        def spread(near, far):
-            crossed = swap_chip(far)
+        weights = (w_gate, w_up, jnp.swapaxes(w_down, 2, 3))
+
+        def launch(units, gate):
+            held = weights if gate is None else lax.optimization_barrier((weights, gate))[0]
+            for layer, c, kind in units:
+                weight = held[kind]
+                piece = lambda base: lax.dynamic_slice(weight, (layer, base * half_experts + c * chunk, 0, 0), (1, chunk) + weight.shape[2:])[0]
+                far = lax.optimization_barrier(piece(1 - chip))
+                near = lax.optimization_barrier(piece(chip))
+                crossed = swap_chip(far)
+                bulk[layer, c, kind] = near, crossed
+
+        def spread(near, crossed):
             return near, swap_core(near), crossed, swap_core(crossed)
 
+        half = rows // 2
+        bulk = {}
+
+        launch([(0, 0, 0), (0, 0, 1), (0, 0, 2)], None)
         residual = hidden_in.astype(jnp.float32)
         for layer in range(num_layers):
             q_w, k_w, v_w = jnp.split(qkv_all[layer], 3, axis=1)
@@ -312,21 +310,35 @@
             residual = residual + jnp.dot(attn_full, out_all[layer], preferred_element_type=jnp.float32)
             normed = rms_norm(residual, gain_mlp[layer])
             far_half = swap_chip(normed)
+            if layer == 0:
+                launch([(0, 1, 0), (0, 1, 1), (0, 1, 2), (1, 0, 0)], normed)
+            else:
+                launch([(1, 1, 1), (1, 1, 2)], normed)
             h_own = gather_mp(normed).astype(jnp.float32)
             h_far = gather_mp(far_half).astype(jnp.float32)
             parts = [None, None]
             for c in range(CHUNKS):
-                gate_parts, up_parts, down_parts = [spread(*exchange(w, layer, c)) for w in (w_gate, w_up, w_down)]
+                gate_parts, up_parts, down_parts = [spread(*bulk[layer, c, kind]) for kind in range(3)]
                 for s, h_rows in enumerate((h_far, h_own)):
                     tables, tokens, gates = routing[s]
                     got = run_experts(h_rows, tables[c], place, tokens, gates, gate_parts, up_parts, down_parts)
                     parts[s] = got if parts[s] is None else parts[s] + got
             far_sum, own_sum = parts
-            pick = lambda value, which: lax.dynamic_slice_in_dim(value, which * rows, rows, 0)
-            from_chip = swap_chip(pick(far_sum, m))
-            from_diagonal = swap_diagonal(pick(far_sum, 1 - m))
-            from_mp = swap_mp(pick(own_sum, 1 - m))
-            residual = residual + pick(own_sum, m) + from_mp + from_chip + from_diagonal
+            pick = lambda value, which, part: lax.dynamic_slice_in_dim(value, which * rows + part * half, half, 0)
+            far_other_1, far_mine_1, far_other_0, far_mine_0 = lax.optimization_barrier(tuple(pick(far_sum, which, part) for which, part in ((1 - m, 1), (m, 1), (1 - m, 0), (m, 0))))
+            via_chip = swap_chip(far_other_1)
+            mine_1 = swap_chip(far_mine_1)
+            via_mp = swap_mp(far_other_0)
+            if layer == 0:
+                launch([(1, 0, 1), (1, 0, 2), (1, 1, 0)], via_mp)
+            sent_0 = lax.optimization_barrier(far_mine_0 + via_mp)
+            mine_0 = swap_chip(sent_0)
+            own_other_0, own_other_1, own_0, own_1 = lax.optimization_barrier(tuple(pick(own_sum, which, part) for which, part in ((1 - m, 0), (1 - m, 1), (m, 0), (m, 1))))
+            other_0 = swap_mp(own_other_0)
+            other_1 = swap_mp(own_other_1 + via_chip)
+            top = own_0 + other_0 + mine_0
+            bottom = own_1 + other_1 + mine_1
+            residual = residual + jnp.concatenate([top, bottom], axis=0)
         return residual
 
-    return jax.shard_map(device_step, mesh=mesh, in_specs=in_specs, out_specs=row_spec, check_vma=False)
+    return jax.shard_map(layers, mesh=mesh, in_specs=in_specs, out_specs=row_spec, check_vma=False)

time: 2930 us -> 2680 us (0.915)
  local copies, waits for them, and re-layouts: 390 us -> 212 us
  waiting for transfers between devices: 1530 us -> 1390 us
  Pallas kernels: 756 us -> 818 us
    ppermute x2 -> x0, waiting for transfers between devices: 273 us -> none  [swap_diagonal(): return lax.ppermute(value, ('mp', 'tok'), [(i, i ^ 6) for i in range(8)])]
    ppermute x12 -> x0, local copies, waits for them, and re-layouts: 95.2 us -> none  [the longest x8 63.4 us: swap_core(): return lax.ppermute(value, 'tok', [(i, i ^ 1) for i in range(4)])]
    squeeze x1 -> x11, local copies, waits for them, and re-layouts: 2.28 us -> 93.4 us  [the longest x10 91.1 us: launch(): lax.dynamic_slice(weight, (layer, base * half_experts + c * chunk, 0, 0),...]
    dynamic_slice x16 -> x6, local copies, waits for them, and re-layouts: 130 us -> 40.8 us  [the longest x4 36.2 us: layers(): lax.dynamic_slice_in_dim(value, which * rows + part * half, half, 0)]
    ppermute x18 -> x22, waiting for transfers between devices: 1050 us -> 1140 us  [swap_chip(): return lax.ppermute(value, 'tok', [(i, i ^ 2) for i in range(4)])]
    pallas_call x2, Pallas kernels: 204 us -> 291 us  [attention(): pl.pallas_call(attention_kernel, grid_spec=grid_spec, out_shape=jax.Shape...]
    slice x9 -> x6, local copies, waits for them, and re-layouts: 83.4 us -> 8.83 us  [the longest x3 6.62 us: layers(): out_all[layer]]
    ppermute x13 -> x17, waiting for transfers between devices: 209 us -> 247 us  [swap_mp(): return lax.ppermute(value, 'mp', [(0, 1), (1, 0)])]
  transfers between devices with their start and end apart: 59 -> 65, of which waited for: 18 -> 20; matrix products, arithmetic and copies ran while one was open for 18% -> 14% of each run, Pallas kernels for 26% -> 31%
where the time goes in v2:
time: 2680 us; the launch traced here: 2670 us
  waiting for transfers between devices  1390 us (52%)
  Pallas kernels  818 us (31%)
  local copies, waits for them, and re-layouts  212 us (8%)
  other arithmetic  183 us (7%)
  starting transfers between devices  48.3 us (2%)
    ppermute x22, waiting for transfers between devices, swap_chip(): return lax.ppermute(value, 'tok', [(i, i ^ 2) for i in range(4)])  1140 us
    pallas_call x8, Pallas kernels, run_experts(): pl.pallas_call(moe_kernel, grid_spec=grid_spec, out_shape=jax.ShapeDtypeS...  491 us
    pallas_call x2, Pallas kernels, attention(): pl.pallas_call(attention_kernel, grid_spec=grid_spec, out_shape=jax.Shape...  291 us
    ppermute x17, waiting for transfers between devices, swap_mp(): return lax.ppermute(value, 'mp', [(0, 1), (1, 0)])  247 us
    squeeze x10, local copies, waits for them, and re-layouts, launch(): lax.dynamic_slice(weight, (layer, base * half_experts + c * chunk, 0, 0),...  91.1 us
    add x4, other arithmetic, layers(): parts[s] = got if parts[s] is None else parts[s] + got  56.4 us
  transfers between devices with their start and end apart: 65, of which 20 were waited for; matrix products, arithmetic and copies ran while one was open for 14% of the time, Pallas kernels for 31%

profile of v2, /device:TPU:0, one launch (start us, length us, event | category | flops | bytes accessed | tf_op | source)
XLA Modules:
  0.0 2673.5 jit_solution(13047519933105824778)
XLA Ops:
  137.7 219.1 %collective-permute-done.26.gate_ref = f32[8200]{0:T(1024)} collective-permute-done((f32[8200]{0:T(1024)}, f32[8200]{0:T(1024)}, u32[]{:S(2)}, u32[]{:S(2)}) %collective-permute-start.26) | collective-permute-done | bytes 32832 | tf_op jit(solution)/shard_map/ppermute | solution.py:224
  387.2 145.8 %attention.2 = bf16[4096,384]{1,0:T(8,128)(2,1)} custom-call(s32[8]{0:T(128)} %and_select_fusion.4.first_ref, bf16[4096,384]{1,0:T(8,128)(2,1)} %get-tuple-element.40.q_ref, bf16[4096,384]{1,0:T(8,128)(2,1)} %get-tuple-element.41.k_ref, bf16[4096,384]{1,0:T(8,128)(2,1)} %get-tuple-element.42.v_ref, s32[4096,1]{1,0:T(8,128)} %copy.111.start_ref), custom_call_target="tpu_custom_call" | custom-call | tf_op jit(solution)/shard_map/attention/pallas_call | solution.py:104
  595.1 39.7 %collective-permute-done.27 = bf16[2048,768]{1,0:T(8,128)(2,1)} collective-permute-done((bf16[2048,768]{1,0:T(8,128)(2,1)}, bf16[2048,768]{1,0:T(8,128)(2,1)}, u32[]{:S(2)}, u32[]{:S(2)}) %collective-permute-start.27) | collective-permute-done | bytes 3145760 | tf_op jit(solution)/shard_map/ppermute | solution.py:224
  634.8 101.1 %collective-permute-done.19.u2 = bf16[8,192,1536]{2,1,0:T(8,128)(2,1)} collective-permute-done((bf16[8,192,1536]{2,1,0:T(8,128)(2,1)}, bf16[8,192,1536]{2,1,0:T(8,128)(2,1)}, u32[]{:S(2)}, u32[]{:S(2)}) %collective-permute-start.19) | collective-permute-done | bytes 4718624 | tf_op jit(solution)/shard_map/ppermute | solution.py:224
  737.4 99.6 %collective-permute-done.22.d2 = bf16[8,192,1536]{2,1,0:T(8,128)(2,1)} collective-permute-done((bf16[8,192,1536]{2,1,0:T(8,128)(2,1)}, bf16[8,192,1536]{2,1,0:T(8,128)(2,1)}, u32[]{:S(2)}, u32[]{:S(2)}) %collective-permute-start.22) | collective-permute-done | bytes 4718624 | tf_op jit(solution)/shard_map/ppermute | solution.py:224
  839.2 98.0 %collective-permute-done.16.g2 = bf16[8,192,1536]{2,1,0:T(8,128)(2,1)} collective-permute-done((bf16[8,192,1536]{2,1,0:T(8,128)(2,1)}, bf16[8,192,1536]{2,1,0:T(8,128)(2,1)}, u32[]{:S(2)}, u32[]{:S(2)}) %collective-permute-start.16) | collective-permute-done | bytes 4718624 | tf_op jit(solution)/shard_map/ppermute | solution.py:224
  959.0 61.7 %experts.10 = f32[4096,768]{1,0:T(8,128)} custom-call(s32[36]{0:T(128)} %compare_select_fusion.3.tile_expert, s32[36]{0:T(128)} %get-tuple-element.86.tile_start, s32[36]{0:T(128)} %get-tuple-element.85.tile_count, s32[2]{0:T(128)} %get-tuple-element.210.place, s32[8200]{0:T(1024)} %slice.110.token_ref, f32[8200]{0:T(1024)} %collective-permute-done.26.gate_ref, ...), custom_call_target="tpu_custom_call" | custom-call | tf_op jit(solution)/shard_map/experts/pallas_call | solution.py:187
  1020.7 61.1 %experts.11 = f32[4096,768]{1,0:T(8,128)} custom-call(s32[36]{0:T(128)} %compare_select_fusion.1.tile_expert, s32[36]{0:T(128)} %get-tuple-element.83.tile_start, s32[36]{0:T(128)} %get-tuple-element.82.tile_count, s32[2]{0:T(128)} %get-tuple-element.211.place, s32[8200]{0:T(1024)} %slice.110.token_ref, f32[8200]{0:T(1024)} %collective-permute-done.26.gate_ref, ...), custom_call_target="tpu_custom_call" | custom-call | tf_op jit(solution)/shard_map/experts/pallas_call | solution.py:187
  1123.0 61.5 %experts.8 = f32[4096,768]{1,0:T(8,128)} custom-call(s32[36]{0:T(128)} %compare_select_fusion.7.tile_expert, s32[36]{0:T(128)} %get-tuple-element.80.tile_start, s32[36]{0:T(128)} %get-tuple-element.79.tile_count, s32[2]{0:T(128)} %get-tuple-element.208.place, s32[8200]{0:T(1024)} %concatenate.85.token_ref, f32[8200]{0:T(1024)} %concatenate.86.gate_ref, ...), custom_call_target="tpu_custom_call" | custom-call | tf_op jit(solution)/shard_map/experts/pallas_call | solution.py:187
  1184.5 61.5 %experts.9 = f32[4096,768]{1,0:T(8,128)} custom-call(s32[36]{0:T(128)} %compare_select_fusion.5.tile_expert, s32[36]{0:T(128)} %get-tuple-element.77.tile_start, s32[36]{0:T(128)} %get-tuple-element.76.tile_count, s32[2]{0:T(128)} %get-tuple-element.209.place, s32[8200]{0:T(1024)} %concatenate.85.token_ref, f32[8200]{0:T(1024)} %concatenate.86.gate_ref, ...), custom_call_target="tpu_custom_call" | custom-call | tf_op jit(solution)/shard_map/experts/pallas_call | solution.py:187
  1281.7 54.8 %collective-permute-done.33 = f32[1024,768]{1,0:T(8,128)S(1)} collective-permute-done((f32[1024,768]{1,0:T(8,128)}, f32[1024,768]{1,0:T(8,128)S(1)}, u32[]{:S(2)}, u32[]{:S(2)}) %collective-permute-start.33) | collective-permute-done | bytes 3145760 | tf_op jit(solution)/shard_map/ppermute | solution.py:224
  1343.4 66.8 %collective-permute-done.24 = f32[1024,768]{1,0:T(8,128)S(1)} collective-permute-done((f32[1024,768]{1,0:T(8,128)S(1)}, f32[1024,768]{1,0:T(8,128)S(1)}, u32[]{:S(2)}, u32[]{:S(2)}) %collective-permute-start.24) | collective-permute-done | bytes 3145760 | tf_op jit(solution)/shard_map/ppermute | solution.py:221
  1419.5 85.6 %collective-permute-done.38.g2 = bf16[8,192,1536]{2,1,0:T(8,128)(2,1)} collective-permute-done((bf16[8,192,1536]{2,1,0:T(8,128)(2,1)}, bf16[8,192,1536]{2,1,0:T(8,128)(2,1)}, u32[]{:S(2)}, u32[]{:S(2)}) %collective-permute-start.38) | collective-permute-done | bytes 4718624 | tf_op jit(solution)/shard_map/ppermute | solution.py:224
  1549.2 145.7 %attention.3 = bf16[4096,384]{1,0:T(8,128)(2,1)} custom-call(s32[8]{0:T(128)} %and_select_fusion.4.first_ref, bf16[4096,384]{1,0:T(8,128)(2,1)} %get-tuple-element.56.q_ref, bf16[4096,384]{1,0:T(8,128)(2,1)} %get-tuple-element.57.k_ref, bf16[4096,384]{1,0:T(8,128)(2,1)} %get-tuple-element.58.v_ref, s32[4096,1]{1,0:T(8,128)} %copy.111.start_ref), custom_call_target="tpu_custom_call" | custom-call | tf_op jit(solution)/shard_map/attention/pallas_call | solution.py:104
  1751.4 59.4 %collective-permute-done.41.u2 = bf16[8,192,1536]{2,1,0:T(8,128)(2,1)} collective-permute-done((bf16[8,192,1536]{2,1,0:T(8,128)(2,1)}, bf16[8,192,1536]{2,1,0:T(8,128)(2,1)}, u32[]{:S(2)}, u32[]{:S(2)}) %collective-permute-start.41) | collective-permute-done | bytes 4718624 | tf_op jit(solution)/shard_map/ppermute | solution.py:224
  1810.8 51.9 %collective-permute-done.44.d2 = bf16[8,192,1536]{2,1,0:T(8,128)(2,1)} collective-permute-done((bf16[8,192,1536]{2,1,0:T(8,128)(2,1)}, bf16[8,192,1536]{2,1,0:T(8,128)(2,1)}, u32[]{:S(2)}, u32[]{:S(2)}) %collective-permute-start.44) | collective-permute-done | bytes 4718624 | tf_op jit(solution)/shard_map/ppermute | solution.py:224
  1865.3 270.4 %collective-permute-done.56 = bf16[2048,768]{1,0:T(8,128)(2,1)S(1)} collective-permute-done((bf16[2048,768]{1,0:T(8,128)(2,1)}, bf16[2048,768]{1,0:T(8,128)(2,1)S(1)}, u32[]{:S(2)}, u32[]{:S(2)}) %collective-permute-start.56) | collective-permute-done | bytes 3145760 | tf_op jit(solution)/shard_map/ppermute | solution.py:224
  2137.2 68.1 %collective-permute-done.57 = bf16[2048,768]{1,0:T(8,128)(2,1)S(1)} collective-permute-done((bf16[2048,768]{1,0:T(8,128)(2,1)S(1)}, bf16[2048,768]{1,0:T(8,128)(2,1)S(1)}, u32[]{:S(2)}, u32[]{:S(2)}) %collective-permute-start.57) | collective-permute-done | bytes 3145760 | tf_op jit(solution)/shard_map/ppermute | solution.py:221
  2211.8 61.8 %experts.14 = f32[4096,768]{1,0:T(8,128)} custom-call(s32[36]{0:T(128)} %compare_select_fusion.3.tile_expert, s32[36]{0:T(128)} %get-tuple-element.86.tile_start, s32[36]{0:T(128)} %get-tuple-element.85.tile_count, s32[2]{0:T(128)} %get-tuple-element.210.place, s32[8200]{0:T(1024)} %slice.110.token_ref, f32[8200]{0:T(1024)} %collective-permute-done.26.gate_ref, ...), custom_call_target="tpu_custom_call" | custom-call | tf_op jit(solution)/shard_map/experts/pallas_call | solution.py:187
  2273.6 61.1 %experts.15 = f32[4096,768]{1,0:T(8,128)} custom-call(s32[36]{0:T(128)} %compare_select_fusion.1.tile_expert, s32[36]{0:T(128)} %get-tuple-element.83.tile_start, s32[36]{0:T(128)} %get-tuple-element.82.tile_count, s32[2]{0:T(128)} %get-tuple-element.211.place, s32[8200]{0:T(1024)} %slice.110.token_ref, f32[8200]{0:T(1024)} %collective-permute-done.26.gate_ref, ...), custom_call_target="tpu_custom_call" | custom-call | tf_op jit(solution)/shard_map/experts/pallas_call | solution.py:187
  2369.9 61.2 %experts.12 = f32[4096,768]{1,0:T(8,128)} custom-call(s32[36]{0:T(128)} %compare_select_fusion.7.tile_expert, s32[36]{0:T(128)} %get-tuple-element.80.tile_start, s32[36]{0:T(128)} %get-tuple-element.79.tile_count, s32[2]{0:T(128)} %get-tuple-element.208.place, s32[8200]{0:T(1024)} %concatenate.85.token_ref, f32[8200]{0:T(1024)} %concatenate.86.gate_ref, ...), custom_call_target="tpu_custom_call" | custom-call | tf_op jit(solution)/shard_map/experts/pallas_call | solution.py:187
  2431.1 61.4 %experts.13 = f32[4096,768]{1,0:T(8,128)} custom-call(s32[36]{0:T(128)} %compare_select_fusion.5.tile_expert, s32[36]{0:T(128)} %get-tuple-element.77.tile_start, s32[36]{0:T(128)} %get-tuple-element.76.tile_count, s32[2]{0:T(128)} %get-tuple-element.209.place, s32[8200]{0:T(1024)} %concatenate.85.token_ref, f32[8200]{0:T(1024)} %concatenate.86.gate_ref, ...), custom_call_target="tpu_custom_call" | custom-call | tf_op jit(solution)/shard_map/experts/pallas_call | solution.py:187
  2525.4 59.4 %collective-permute-done.62 = f32[1024,768]{1,0:T(8,128)S(1)} collective-permute-done((f32[1024,768]{1,0:T(8,128)}, f32[1024,768]{1,0:T(8,128)S(1)}, u32[]{:S(2)}, u32[]{:S(2)}) %collective-permute-start.62) | collective-permute-done | bytes 3145760 | tf_op jit(solution)/shard_map/ppermute | solution.py:224
  2593.3 65.2 %collective-permute-done.55 = f32[1024,768]{1,0:T(8,128)S(1)} collective-permute-done((f32[1024,768]{1,0:T(8,128)S(1)}, f32[1024,768]{1,0:T(8,128)S(1)}, u32[]{:S(2)}, u32[]{:S(2)}) %collective-permute-start.55) | collective-permute-done | bytes 3145760 | tf_op jit(solution)/shard_map/ppermute | solution.py:221
  (345 shorter events, 537.3 us)
Async XLA Ops:
  13.7 522.9 %all-gather.5.cloned.1.call-start = ((), (), s32[]{:S(2)}) async-start(), calls=%async_computation.1 | async-start | bytes 2654208 | tf_op jit(solution)/shard_map/all_gather | solution.py:250
  31.2 503.4 %collective-permute-start.13 = (bf16[8,192,1536]{2,1,0:T(8,128)(2,1)}, bf16[8,192,1536]{2,1,0:T(8,128)(2,1)}, u32[]{:S(2)}, u32[]{:S(2)}) collective-permute-start(bf16[8,192,1536]{2,1,0:T(8,128)(2,1)} %get-tuple-element.124), channel_id=1, source_target_pairs={{0,2},{1,3},{2,0},{3,1},{4,6},{5,7},{6,4},{7,5}} | collective-permute-start | bytes 14155784 | tf_op jit(solution)/shard_map/ppermute | solution.py:224
  48.8 506.9 %collective-permute-start.12 = (bf16[8,192,1536]{2,1,0:T(8,128)(2,1)}, bf16[8,192,1536]{2,1,0:T(8,128)(2,1)}, u32[]{:S(2)}, u32[]{:S(2)}) collective-permute-start(bf16[8,192,1536]{2,1,0:T(8,128)(2,1)} %get-tuple-element.125.d0), channel_id=1, source_target_pairs={{0,1},{1,0},{2,3},{3,2},{4,5},{5,4},{6,7},{7,6}} | collective-permute-start | bytes 14155784 | tf_op jit(solution)/shard_map/ppermute | solution.py:227
  65.8 490.4 %collective-permute-start.10 = (bf16[8,192,1536]{2,1,0:T(8,128)(2,1)}, bf16[8,192,1536]{2,1,0:T(8,128)(2,1)}, u32[]{:S(2)}, u32[]{:S(2)}) collective-permute-start(bf16[8,192,1536]{2,1,0:T(8,128)(2,1)} %get-tuple-element.126), channel_id=1, source_target_pairs={{0,2},{1,3},{2,0},{3,1},{4,6},{5,7},{6,4},{7,5}} | collective-permute-start | bytes 14155784 | tf_op jit(solution)/shard_map/ppermute | solution.py:224
  71.5 484.8 %collective-permute-start.7 = (bf16[8,192,1536]{2,1,0:T(8,128)(2,1)}, bf16[8,192,1536]{2,1,0:T(8,128)(2,1)}, u32[]{:S(2)}, u32[]{:S(2)}) collective-permute-start(bf16[8,192,1536]{2,1,0:T(8,128)(2,1)} %get-tuple-element.213), channel_id=1, source_target_pairs={{0,2},{1,3},{2,0},{3,1},{4,6},{5,7},{6,4},{7,5}} | collective-permute-start | bytes 14155784 | tf_op jit(solution)/shard_map/ppermute | solution.py:224
  101.7 255.1 %collective-permute-start.26 = (f32[8200]{0:T(1024)}, f32[8200]{0:T(1024)}, u32[]{:S(2)}, u32[]{:S(2)}) collective-permute-start(f32[8200]{0:T(1024)} %concatenate.86.gate_ref), channel_id=1, source_target_pairs={{0,2},{1,3},{2,0},{3,1},{4,6},{5,7},{6,4},{7,5}} | collective-permute-start | bytes 98408 | tf_op jit(solution)/shard_map/ppermute | solution.py:224
  361.1 202.4 %collective-permute-start.9 = (bf16[8,192,1536]{2,1,0:T(8,128)(2,1)}, bf16[8,192,1536]{2,1,0:T(8,128)(2,1)}, u32[]{:S(2)}, u32[]{:S(2)}) collective-permute-start(bf16[8,192,1536]{2,1,0:T(8,128)(2,1)} %get-tuple-element.127.u0), channel_id=1, source_target_pairs={{0,1},{1,0},{2,3},{3,2},{4,5},{5,4},{6,7},{7,6}} | collective-permute-start | bytes 14155784 | tf_op jit(solution)/shard_map/ppermute | solution.py:227
  594.6 242.4 %collective-permute-start.22 = (bf16[8,192,1536]{2,1,0:T(8,128)(2,1)}, bf16[8,192,1536]{2,1,0:T(8,128)(2,1)}, u32[]{:S(2)}, u32[]{:S(2)}) collective-permute-start(bf16[8,192,1536]{2,1,0:T(8,128)(2,1)} %get-tuple-element.120), channel_id=1, source_target_pairs={{0,2},{1,3},{2,0},{3,1},{4,6},{5,7},{6,4},{7,5}} | collective-permute-start | bytes 14155784 | tf_op jit(solution)/shard_map/ppermute | solution.py:224
  594.6 242.4 %collective-permute-start.21 = (bf16[8,192,1536]{2,1,0:T(8,128)(2,1)S(1)}, bf16[8,192,1536]{2,1,0:T(8,128)(2,1)S(1)}, u32[]{:S(2)}, u32[]{:S(2)}) collective-permute-start(bf16[8,192,1536]{2,1,0:T(8,128)(2,1)S(1)} %get-tuple-element.121.d0), channel_id=1, source_target_pairs={{0,1},{1,0},{2,3},{3,2},{4,5},{5,4},{6,7},{7,6}} | collective-permute-start | bytes 14155784 | tf_op jit(solution)/shard_map/ppermute | solution.py:227
  634.8 302.4 %collective-permute-start.16 = (bf16[8,192,1536]{2,1,0:T(8,128)(2,1)}, bf16[8,192,1536]{2,1,0:T(8,128)(2,1)}, u32[]{:S(2)}, u32[]{:S(2)}) collective-permute-start(bf16[8,192,1536]{2,1,0:T(8,128)(2,1)} %get-tuple-element.118), channel_id=1, source_target_pairs={{0,2},{1,3},{2,0},{3,1},{4,6},{5,7},{6,4},{7,5}} | collective-permute-start | bytes 14155784 | tf_op jit(solution)/shard_map/ppermute | solution.py:224
  735.9 209.5 %collective-permute-start.28 = (bf16[2048,768]{1,0:T(8,128)(2,1)}, bf16[2048,768]{1,0:T(8,128)(2,1)}, u32[]{:S(2)}, u32[]{:S(2)}) collective-permute-start(bf16[2048,768]{1,0:T(8,128)(2,1)} %collective-permute-done.27), channel_id=1, source_target_pairs={{0,4},{4,0},{1,5},{5,1},{2,6},{6,2},{3,7},{7,3}} | collective-permute-start | bytes 9437192 | tf_op jit(solution)/shard_map/ppermute | solution.py:221
  737.4 283.3 %collective-permute-start.15 = (bf16[8,192,1536]{2,1,0:T(8,128)(2,1)}, bf16[8,192,1536]{2,1,0:T(8,128)(2,1)}, u32[]{:S(2)}, u32[]{:S(2)}) collective-permute-start(bf16[8,192,1536]{2,1,0:T(8,128)(2,1)} %get-tuple-element.119.g0), channel_id=1, source_target_pairs={{0,1},{1,0},{2,3},{3,2},{4,5},{5,4},{6,7},{7,6}} | collective-permute-start | bytes 14155784 | tf_op jit(solution)/shard_map/ppermute | solution.py:227
  837.0 183.7 %collective-permute-start.20 = (bf16[8,192,1536]{2,1,0:T(8,128)(2,1)}, bf16[8,192,1536]{2,1,0:T(8,128)(2,1)}, u32[]{:S(2)}, u32[]{:S(2)}) collective-permute-start(bf16[8,192,1536]{2,1,0:T(8,128)(2,1)} %collective-permute-done.19.u2), channel_id=1, source_target_pairs={{0,1},{1,0},{2,3},{3,2},{4,5},{5,4},{6,7},{7,6}} | collective-permute-start | bytes 14155784 | tf_op jit(solution)/shard_map/ppermute | solution.py:227
  837.1 183.7 %collective-permute-start.23 = (bf16[8,192,1536]{2,1,0:T(8,128)(2,1)}, bf16[8,192,1536]{2,1,0:T(8,128)(2,1)}, u32[]{:S(2)}, u32[]{:S(2)}) collective-permute-start(bf16[8,192,1536]{2,1,0:T(8,128)(2,1)} %collective-permute-done.22.d2), channel_id=1, source_target_pairs={{0,1},{1,0},{2,3},{3,2},{4,5},{5,4},{6,7},{7,6}} | collective-permute-start | bytes 14155784 | tf_op jit(solution)/shard_map/ppermute | solution.py:227
  1280.1 224.9 %collective-permute-start.38 = (bf16[8,192,1536]{2,1,0:T(8,128)(2,1)}, bf16[8,192,1536]{2,1,0:T(8,128)(2,1)}, u32[]{:S(2)}, u32[]{:S(2)}) collective-permute-start(bf16[8,192,1536]{2,1,0:T(8,128)(2,1)} %get-tuple-element.116), channel_id=1, source_target_pairs={{0,2},{1,3},{2,0},{3,1},{4,6},{5,7},{6,4},{7,5}} | collective-permute-start | bytes 14155784 | tf_op jit(solution)/shard_map/ppermute | solution.py:224
  1417.7 288.1 %collective-permute-start.37 = (bf16[8,192,1536]{2,1,0:T(8,128)(2,1)}, bf16[8,192,1536]{2,1,0:T(8,128)(2,1)}, u32[]{:S(2)}, u32[]{:S(2)}) collective-permute-start(bf16[8,192,1536]{2,1,0:T(8,128)(2,1)} %get-tuple-element.117.g0), channel_id=1, source_target_pairs={{0,1},{1,0},{2,3},{3,2},{4,5},{5,4},{6,7},{7,6}} | collective-permute-start | bytes 14155784 | tf_op jit(solution)/shard_map/ppermute | solution.py:227
  1505.1 200.7 %collective-permute-start.39 = (bf16[8,192,1536]{2,1,0:T(8,128)(2,1)}, bf16[8,192,1536]{2,1,0:T(8,128)(2,1)}, u32[]{:S(2)}, u32[]{:S(2)}) collective-permute-start(bf16[8,192,1536]{2,1,0:T(8,128)(2,1)} %collective-permute-done.38.g2), channel_id=1, source_target_pairs={{0,1},{1,0},{2,3},{3,2},{4,5},{5,4},{6,7},{7,6}} | collective-permute-start | bytes 14155784 | tf_op jit(solution)/shard_map/ppermute | solution.py:227
  1516.4 191.4 %collective-permute-start.47 = (bf16[8,192,1536]{2,1,0:T(8,128)(2,1)}, bf16[8,192,1536]{2,1,0:T(8,128)(2,1)}, u32[]{:S(2)}, u32[]{:S(2)}) collective-permute-start(bf16[8,192,1536]{2,1,0:T(8,128)(2,1)} %get-tuple-element.110), channel_id=1, source_target_pairs={{0,2},{1,3},{2,0},{3,1},{4,6},{5,7},{6,4},{7,5}} | collective-permute-start | bytes 14155784 | tf_op jit(solution)/shard_map/ppermute | solution.py:224
  1517.9 190.0 %collective-permute-start.46 = (bf16[8,192,1536]{2,1,0:T(8,128)(2,1)}, bf16[8,192,1536]{2,1,0:T(8,128)(2,1)}, u32[]{:S(2)}, u32[]{:S(2)}) collective-permute-start(bf16[8,192,1536]{2,1,0:T(8,128)(2,1)} %get-tuple-element.111.g0), channel_id=1, source_target_pairs={{0,1},{1,0},{2,3},{3,2},{4,5},{5,4},{6,7},{7,6}} | collective-permute-start | bytes 14155784 | tf_op jit(solution)/shard_map/ppermute | solution.py:227
  1810.8 325.4 %collective-permute-start.42 = (bf16[8,192,1536]{2,1,0:T(8,128)(2,1)}, bf16[8,192,1536]{2,1,0:T(8,128)(2,1)}, u32[]{:S(2)}, u32[]{:S(2)}) collective-permute-start(bf16[8,192,1536]{2,1,0:T(8,128)(2,1)} %collective-permute-done.41.u2), channel_id=1, source_target_pairs={{0,1},{1,0},{2,3},{3,2},{4,5},{5,4},{6,7},{7,6}} | collective-permute-start | bytes 14155784 | tf_op jit(solution)/shard_map/ppermute | solution.py:227
  1862.7 273.5 %collective-permute-start.45 = (bf16[8,192,1536]{2,1,0:T(8,128)(2,1)}, bf16[8,192,1536]{2,1,0:T(8,128)(2,1)}, u32[]{:S(2)}, u32[]{:S(2)}) collective-permute-start(bf16[8,192,1536]{2,1,0:T(8,128)(2,1)} %collective-permute-done.44.d2), channel_id=1, source_target_pairs={{0,1},{1,0},{2,3},{3,2},{4,5},{5,4},{6,7},{7,6}} | collective-permute-start | bytes 14155784 | tf_op jit(solution)/shard_map/ppermute | solution.py:227
  1862.7 274.0 %collective-permute-start.50 = (bf16[8,192,1536]{2,1,0:T(8,128)(2,1)}, bf16[8,192,1536]{2,1,0:T(8,128)(2,1)}, u32[]{:S(2)}, u32[]{:S(2)}) collective-permute-start(bf16[8,192,1536]{2,1,0:T(8,128)(2,1)} %get-tuple-element.108), channel_id=1, source_target_pairs={{0,2},{1,3},{2,0},{3,1},{4,6},{5,7},{6,4},{7,5}} | collective-permute-start | bytes 14155784 | tf_op jit(solution)/shard_map/ppermute | solution.py:224
  1863.2 273.5 %collective-permute-start.53 = (bf16[8,192,1536]{2,1,0:T(8,128)(2,1)}, bf16[8,192,1536]{2,1,0:T(8,128)(2,1)}, u32[]{:S(2)}, u32[]{:S(2)}) collective-permute-start(bf16[8,192,1536]{2,1,0:T(8,128)(2,1)} %get-tuple-element.106), channel_id=1, source_target_pairs={{0,2},{1,3},{2,0},{3,1},{4,6},{5,7},{6,4},{7,5}} | collective-permute-start | bytes 14155784 | tf_op jit(solution)/shard_map/ppermute | solution.py:224
  1864.7 270.9 %collective-permute-start.56 = (bf16[2048,768]{1,0:T(8,128)(2,1)}, bf16[2048,768]{1,0:T(8,128)(2,1)S(1)}, u32[]{:S(2)}, u32[]{:S(2)}) collective-permute-start(bf16[2048,768]{1,0:T(8,128)(2,1)} %multiply_convert_fusion), channel_id=1, source_target_pairs={{0,2},{1,3},{2,0},{3,1},{4,6},{5,7},{6,4},{7,5}} | collective-permute-start | bytes 9437192 | tf_op jit(solution)/shard_map/ppermute | solution.py:224
  (77 other events, 5522.3 us)
Sparse Core Ops, SparseCore 0:
  13.9 40.1 all-gather.2
  55.9 32.6 all-gather.4
